TPU v7x, 512 devices: a whole 4x8x8 slice. The times are simulated.
512 devices in a mesh: member: 8 (over y_hi, x), space: 64 (over z, y_lo, core).
Axes of the slice: x: 4, y: 8 (y_hi: 2, y_lo: 4; y = y_hi * 4 + y_lo), z: 8, core: 2. Of those that a mesh axis runs over, the one named last changes fastest.
Arguments:
- node_states: bfloat16 [16384, 1024], P('space'), may hold values from -6 to 6
- noise: bfloat16 [8, 16, 16384], P('member', None, 'space'), may hold values from -4 to 4
- norm_gain: float32 [1024], replicated, may hold values from 0.5 to 1.5
- cond_weight: bfloat16 [16, 2048], replicated, may hold values from -1.5 to 1.5
- w_query: bfloat16 [1024, 1024], P('space'), may hold values from -0.1875 to 0.1875
- w_key: bfloat16 [1024, 1024], P('space'), may hold values from -0.1875 to 0.1875
- w_value: bfloat16 [1024, 1024], P('space'), may hold values from -0.1875 to 0.1875
- w_out: bfloat16 [1024, 1024], P('space'), may hold values from -0.1875 to 0.1875
- edge_src: int32 [8, 16384], P(None, 'space'), may hold values from 0 to 511, as said below
- send_rows: int32 [16384], P('space'), may hold values from 0 to 255, as said below
- dec_src: int32 [3, 65536], P(None, 'space'), may hold values from 0 to 255
- dec_weight: float32 [3, 65536], P(None, 'space'), may hold values from 0.2 to 1
- w_decode: bfloat16 [100, 1024], replicated, may hold values from -0.1875 to 0.1875
- truth: bfloat16 [100, 65536], P(None, 'space'), may hold values from -6 to 6
- area: float32 [65536], P('space'), may hold values from 0.1 to 3.5
Outputs:
- loss: float32 [], replicated
- field_grad: bfloat16 [8, 100, 65536], P('member', None, 'space')
Inputs may be any that keep to these rules, and one draw needn't show every extreme that they name: `send_rows`: each block's 2 * 128 entries are distinct node indices within that block. `edge_src`: entries below 128 name a row of the previous block's halo rows, entries from 384 on a row of the next block's; of each such halo half only a leading part of at least 64 rows is named, its length varying by block, and in some block the whole half is named.
All inputs are finite; a program needn't handle non-finite values.
Results may differ from a plain program's by a relative error of at most 0.015.
Values may be sent and summed in bfloat16 or wider, within the bound.
A program may use at most 64 MiB of HBM per device.

v0:
```python
import functools

import jax
import jax.numpy as jnp
from jax import lax
from jax.sharding import Mesh
from jax.sharding import PartitionSpec as P

HEADS = 16
SPACE = ("space_0", "space_1", "space_2")
MEMBER = ("member_0", "member_1")
MEMBER_SPACE = ("member_0", "member_1", "space_0", "space_1", "space_2")


SMOOTH = 0.25
EPS = 1e-05


def extended(block, sides, width):
    for axis, dim in sides:
        count = lax.axis_size(axis)
        forward = [(i, i + 1) for i in range(count - 1)]
        forward.append((count - 1, 0))
        backward = [(target, source) for source, target in forward]
        low = lax.ppermute(
            lax.slice_in_dim(block, block.shape[dim] - width, None, axis=dim), axis, forward
        )
        high = lax.ppermute(lax.slice_in_dim(block, 0, width, axis=dim), axis, backward)
        block = jnp.concatenate([low, block, high], axis=dim)
    return block


def in_one_piece(arrays, axis, dim, along):
    both = jnp.concatenate(arrays, axis=along)
    whole, at, finished = (lax.all_gather(both, axis, axis=dim, tiled=True), 0, [])
    for a in arrays:
        finished.append(lax.slice_in_dim(whole, at, at + a.shape[along], axis=along))
        at += a.shape[along]
    return tuple(finished)


def from_everyone(shard, axis):
    copies = jnp.broadcast_to(shard, (lax.axis_size(axis), *shard.shape))
    return lax.all_to_all(copies, axis, split_axis=0, concat_axis=0, tiled=True)


def in_order(blocks, dim):
    lengths = list(blocks.shape[1:])
    lengths[dim] *= blocks.shape[0]
    return jnp.moveaxis(blocks, 0, dim).reshape(lengths)


def collect(shard, axis, dim):
    blocks = from_everyone(shard, axis)
    return in_order(blocks, dim)


def by_axis(shard, axes):
    return functools.reduce(lax.psum, axes, shard)


def condition(states, noise_block, norm_gain, cond_weight):
    values = states.astype(jnp.float32)
    center = values - jnp.mean(values, axis=1, keepdims=True)
    spread = jnp.mean(center * center, axis=1, keepdims=True)
    normed = center * lax.rsqrt(spread + EPS)
    terms = lax.dot_general(
        noise_block, cond_weight, (((0,), (0,)), ((), ())), preferred_element_type=jnp.float32
    )
    model_width = states.shape[1]
    return (normed * norm_gain * (1.0 + terms[:, :model_width]) + terms[:, model_width:]).astype(
        jnp.bfloat16
    )


def attention(query_rows, key_ext, value_ext, sources):
    row_count, model_width = query_rows.shape
    head_size = model_width // HEADS
    factor = 1.0 / head_size**0.5
    query_wide = query_rows.astype(jnp.float32).reshape(row_count, HEADS, head_size)
    numerator = jnp.zeros((row_count, HEADS, head_size), jnp.float32)
    denominator = jnp.zeros((row_count, HEADS), jnp.float32)
    for slot_index in range(sources.shape[0]):
        picked = sources[slot_index]
        gathered_key = key_ext[picked].astype(jnp.float32).reshape(row_count, HEADS, head_size)
        weight = jnp.exp(jnp.sum(query_wide * gathered_key, axis=2) * factor)
        gathered_value = value_ext[picked].astype(jnp.float32).reshape(row_count, HEADS, head_size)
        numerator = numerator + weight[:, :, None] * gathered_value
        denominator = denominator + weight
    return (
        (numerator / denominator[:, :, None]).reshape(row_count, model_width).astype(jnp.bfloat16)
    )


def decode(processed, sources, dec_weight, w_decode):
    gathered = jnp.zeros((sources.shape[1], processed.shape[1]), jnp.float32)
    for neighbour in range(sources.shape[0]):
        gathered = gathered + dec_weight[neighbour][:, None] * processed[sources[neighbour]].astype(
            jnp.float32
        )
    return lax.dot_general(
        w_decode,
        gathered.astype(jnp.bfloat16),
        (((1,), (1,)), ((), ())),
        preferred_element_type=jnp.float32,
    ).astype(jnp.bfloat16)


def smooth_abs(difference):
    return jnp.sqrt(difference * difference + SMOOTH * SMOOTH)


def per_device(
    node_states,
    noise,
    norm_gain,
    cond_weight,
    w_query,
    w_key,
    w_value,
    w_out,
    edge_src,
    send_rows,
    dec_src,
    dec_weight,
    w_decode,
    truth,
    area,
):
    hidden = condition(node_states, noise[0], norm_gain, cond_weight)
    halo_rows = send_rows.shape[0] // 2
    padded = extended(hidden[send_rows], ((SPACE, 0),), halo_rows)
    kv_input = jnp.concatenate((padded[:halo_rows], hidden, padded[3 * halo_rows :]), axis=0)
    whole_query, whole_key, whole_value = in_one_piece((w_query, w_key, w_value), SPACE, 0, 1)
    query_rows = jnp.dot(hidden, whole_query, preferred_element_type=jnp.float32).astype(
        jnp.bfloat16
    )
    key_rows = jnp.dot(kv_input, whole_key, preferred_element_type=jnp.float32).astype(jnp.bfloat16)
    value_rows = jnp.dot(kv_input, whole_value, preferred_element_type=jnp.float32).astype(
        jnp.bfloat16
    )
    key_ext, value_ext = (key_rows, value_rows)
    attended = attention(query_rows, key_ext, value_ext, edge_src)
    whole_out = collect(w_out, SPACE, 0)
    update = jnp.dot(attended, whole_out, preferred_element_type=jnp.float32)
    processed = (node_states.astype(jnp.float32) + update).astype(jnp.bfloat16)
    fields = decode(processed, dec_src, dec_weight, w_decode)
    truth_wide = truth.astype(jnp.float32)
    members = lax.axis_size(MEMBER)
    pair_norm = 2.0 * members * (members - 1)
    columns = fields.shape[1] // members
    offset = lax.axis_index(MEMBER) * columns
    grouped = lax.all_to_all(fields[None], MEMBER, split_axis=2, concat_axis=0, tiled=True)
    truth_part = lax.dynamic_slice_in_dim(truth_wide, offset, columns, 1)
    area_part = lax.dynamic_slice_in_dim(area, offset, columns, 0)
    values = grouped.astype(jnp.float32)
    skill_gap = values - truth_part[None]
    skill_abs = smooth_abs(skill_gap)
    spread_abs = jnp.zeros_like(values)
    spread_slope = jnp.zeros_like(values)
    for other_member in range(members):
        difference = values - values[other_member][None]
        magnitude = smooth_abs(difference)
        spread_abs = spread_abs + magnitude
        spread_slope = spread_slope + difference / magnitude
    crps_value = (
        jnp.sum(skill_abs, axis=0) / members
        - (jnp.sum(spread_abs, axis=0) - members * SMOOTH) / pair_norm
    )
    local_sum = jnp.sum(area_part[None, :] * crps_value)
    member_slope = (
        area_part[None, None, :] * (skill_gap / skill_abs - spread_slope / (members - 1))
    ).astype(jnp.bfloat16)
    field_grad = lax.all_to_all(member_slope, MEMBER, split_axis=0, concat_axis=2, tiled=True)
    loss_sum = by_axis(local_sum, MEMBER_SPACE)
    loss = loss_sum / (truth.shape[0] * truth.shape[1] * lax.axis_size(SPACE))
    return (loss, field_grad)


def solution(mesh):
    split = Mesh(
        mesh.devices.reshape(2, 4, 8, 4, 2),
        ("member_0", "member_1", "space_0", "space_1", "space_2"),
    )
    return jax.shard_map(
        per_device,
        mesh=split,
        in_specs=(
            P(SPACE, None),
            P(MEMBER, None, SPACE),
            P(),
            P(),
            P(SPACE, None),
            P(SPACE, None),
            P(SPACE, None),
            P(SPACE, None),
            P(None, SPACE),
            P(SPACE),
            P(None, SPACE),
            P(None, SPACE),
            P(),
            P(None, SPACE),
            P(SPACE),
        ),
        out_specs=(P(), P(MEMBER, None, SPACE)),
        check_vma=False,
    )
```

profile of v0, /device:TPU:1, one launch (start us, length us, event | category | flops | bytes accessed | tf_op | source)
XLA Modules:
  0.0 375.8 jit_solution(14618342480510952781)
XLA Ops:
  14.9 4.6 %collective-permute-start = (bf16[128,1024]{1,0:T(8,128)(2,1)S(1)}, bf16[128,1024]{1,0:T(8,128)(2,1)S(1)}, u32[]{:S(2)}, u32[]{:S(2)}) collective-permute-start(bf16[128,1024]{1,0:T(8,128)(2,1)S(1)} %get-tuple-element.13), channel_id=1, source_target_pairs={{0,1},{1,2},{2,3},{3,4},{4,5},{5,6},{6,7},{7,8},{8,9},{9,10},{10,1... | collective-permute-start | bytes 786440 | tf_op jit(solution)/shard_map/ppermute | solution.py:25
  19.5 6.1 %collective-permute-start.1 = (bf16[128,1024]{1,0:T(8,128)(2,1)S(1)}, bf16[128,1024]{1,0:T(8,128)(2,1)S(1)}, u32[]{:S(2)}, u32[]{:S(2)}) collective-permute-start(bf16[128,1024]{1,0:T(8,128)(2,1)S(1)} %get-tuple-element.14), channel_id=1, source_target_pairs={{1,0},{2,1},{3,2},{4,3},{5,4},{6,5},{7,6},{8,7},{9,8},{10,9},{11,1... | collective-permute-start | bytes 786440 | tf_op jit(solution)/shard_map/ppermute | solution.py:28
  27.3 11.6 %all-to-all-start = ((bf16[64,16,1024]{2,1,0:T(8,128)(2,1)}), bf16[64,16,1024]{2,1,0:T(8,128)(2,1)}, u32[]{:S(2)}, u32[]{:S(2)}) async-start(bf16[64,16,1024]{2,1,0:T(8,128)(2,1)} %broadcast_in_dim.7), calls=%async_computation | async-start | bytes 4194304 | tf_op jit(solution)/shard_map/all_to_all | solution.py:44
  39.2 135.5 %all-gather.2.cloned.1.call-done = bf16[1024,3072]{1,0:T(8,128)(2,1)} async-done(((bf16[16,3072]{1,0:T(8,128)(2,1)}), bf16[1024,3072]{1,0:T(8,128)(2,1)}) %all-gather.2.cloned.1.call-update) | async-done | bytes 6291472 | tf_op jit(solution)/shard_map/all_gather | solution.py:35
  174.7 2.8 fusion.7
  177.6 2.0 gather_fusion.5
  179.5 2.0 gather_fusion.7
  181.5 3.0 fusion.10
  184.5 2.0 gather_fusion.6
  188.5 2.0 gather_fusion.9
  190.4 2.0 gather_fusion.10
  192.4 2.0 gather_fusion.11
  194.4 2.0 gather_fusion.12
  196.4 2.0 gather_fusion.13
  198.4 2.0 gather_fusion.14
  200.3 2.0 gather_fusion.15
  202.3 2.0 gather_fusion.16
  204.2 2.0 gather_fusion.1
  206.2 2.0 gather_fusion.2
  208.2 2.0 gather_fusion.3
  210.2 2.2 gather_fusion.4
  212.4 2.5 fusion.14
  215.1 3.3 convert_multiply_fusion
  218.5 2.5 copy.96
  221.0 2.6 copy.98
  223.6 2.5 copy.100
  226.1 2.5 copy.102
  228.7 2.5 copy.104
  231.2 2.6 copy.106
  238.0 2.2 copy.101
  241.4 2.3 copy.105
  243.7 2.2 copy.107
  247.2 2.2 copy.95
  257.8 2.3 fusion.13
  260.1 4.1 %gather_fusion.17 = bf16[1024,1024]{1,0:T(8,128)(2,1)S(1)} fusion(bf16[256,1024]{1,0:T(8,128)(2,1)S(1)} %fusion.13, s32[1024]{0:T(1024)S(1)} %broadcast_clamp_fusion.2), kind=kCustom, calls=%fused_computation.17 | custom fusion | bytes 4198400 | tf_op jit(solution)/shard_map/gather | solution.py:98
  264.2 5.4 %gather_fusion.18 = bf16[1024,1024]{1,0:T(8,128)(2,1)} fusion(bf16[256,1024]{1,0:T(8,128)(2,1)S(1)} %fusion.13, s32[1024]{0:T(1024)S(1)} %broadcast_clamp_fusion.1), kind=kCustom, calls=%fused_computation.18 | custom fusion | bytes 4198400 | tf_op jit(solution)/shard_map/gather | solution.py:98
  269.6 5.4 %gather_fusion.19 = bf16[1024,1024]{1,0:T(8,128)(2,1)} fusion(bf16[256,1024]{1,0:T(8,128)(2,1)S(1)} %fusion.13, s32[1024]{0:T(1024)S(1)} %broadcast_clamp_fusion), kind=kCustom, calls=%fused_computation.19 | custom fusion | bytes 4198400 | tf_op jit(solution)/shard_map/gather | solution.py:98
  274.9 3.7 fusion.20
  279.8 2.3 reduce
  283.5 8.2 %all-to-all-start.1 = ((bf16[8,2,6400]{2,1,0:T(2,128)(2,1)}), bf16[8,2,6400]{2,1,0:T(2,128)(2,1)S(1)}, u32[]{:S(2)}, u32[]{:S(2)}) async-start(bf16[8,2,6400]{2,1,0:T(2,128)(2,1)} %reshape.717), calls=%async_computation.1 | async-start | bytes 409600 | tf_op jit(solution)/shard_map/all_to_all | solution.py:153
  293.3 8.3 %all-to-all-done.1 = bf16[8,2,6400]{2,1,0:T(2,128)(2,1)S(1)} async-done(((bf16[8,2,6400]{2,1,0:T(2,128)(2,1)}), bf16[8,2,6400]{2,1,0:T(2,128)(2,1)S(1)}, u32[]{:S(2)}, u32[]{:S(2)}) %all-to-all-start.1) | async-done | bytes 204832 | tf_op jit(solution)/shard_map/all_to_all | solution.py:153
  305.1 2.2 fusion.26
  308.0 3.4 all-to-all-start.2
  312.0 8.3 %psum.35 = f32[]{:T(128)} all-reduce(f32[]{:T(128)} %multiply_reduce_fusion), channel_id=1, replica_groups=mesh['member_0'=2,'member_1'=4,'space_0'=8,'space_1'=4,'space_2'=2] {'me..., use_global_device_ids=true, to_apply=%region_13.0 | all-reduce | flops 1 | bytes 8 | tf_op jit(solution)/shard_map/psum | solution.py:59
  320.3 9.5 %psum.36 = f32[]{:T(128)} all-reduce(f32[]{:T(128)} %psum.35), channel_id=1, replica_groups=mesh['member_0'=2,'member_1'=4,'space_0'=8,'space_1'=4,'space_2'=2] {'me..., use_global_device_ids=true, to_apply=%region_14.0 | all-reduce | flops 1 | bytes 8 | tf_op jit(solution)/shard_map/psum | solution.py:59
  329.8 12.4 %psum.37 = f32[]{:T(128)} all-reduce(f32[]{:T(128)} %psum.36), channel_id=1, replica_groups=mesh['member_0'=2,'member_1'=4,'space_0'=8,'space_1'=4,'space_2'=2] {'sp..., use_global_device_ids=true, to_apply=%region_15.0 | all-reduce | flops 1 | bytes 8 | tf_op jit(solution)/shard_map/psum | solution.py:59
  342.2 12.0 %psum.38 = f32[]{:T(128)} all-reduce(f32[]{:T(128)} %psum.37), channel_id=1, replica_groups=mesh['member_0'=2,'member_1'=4,'space_0'=8,'space_1'=4,'space_2'=2] {'sp..., use_global_device_ids=true, to_apply=%region_16.0 | all-reduce | flops 1 | bytes 8 | tf_op jit(solution)/shard_map/psum | solution.py:59
  354.2 12.1 %psum.39 = f32[]{:T(128)} all-reduce(f32[]{:T(128)} %psum.38), channel_id=1, replica_groups=mesh['member_0'=2,'member_1'=4,'space_0'=8,'space_1'=4,'space_2'=2] {'sp..., use_global_device_ids=true, to_apply=%region_17.0 | all-reduce | flops 1 | bytes 8 | tf_op jit(solution)/shard_map/psum | solution.py:59
  (122 shorter events, 36.1 us)
Async XLA Ops:
  7.2 267.8 %copy-start = (bf16[100,1024]{1,0:T(8,128)(2,1)S(1)}, bf16[100,1024]{1,0:T(8,128)(2,1)}, u32[]{:S(2)}) copy-start(bf16[100,1024]{1,0:T(8,128)(2,1)} %param.27) | copy-start | bytes 614404
  7.2 6.1 %copy-start.1 = (bf16[256,1024]{1,0:T(8,128)(2,1)S(1)}, bf16[256,1024]{1,0:T(8,128)(2,1)}, u32[]{:S(2)}) copy-start(bf16[256,1024]{1,0:T(8,128)(2,1)} %param.15) | copy-start | bytes 1572868
  7.2 6.1 %copy-start.25 = (f32[1024]{0:T(1024)S(1)}, f32[1024]{0:T(1024)}, u32[]{:S(2)}) copy-start(f32[1024]{0:T(1024)} %param.17) | copy-start | bytes 12292
  7.2 167.5 %all-gather.2.cloned.1.call-start = ((), (), s32[]{:S(2)}) async-start(), calls=%async_computation.3 | async-start | bytes 6389760 | tf_op jit(solution)/shard_map/all_gather | solution.py:35
  13.7 11.9 %copy-start.21 = (bf16[16,1024]{1,0:T(8,128)(2,1)S(1)}, bf16[16,1024]{1,0:T(8,128)(2,1)}, u32[]{:S(2)}) copy-start(bf16[16,1024]{1,0:T(8,128)(2,1)} %param.22) | copy-start | bytes 98308
  14.9 24.2 %collective-permute-start = (bf16[128,1024]{1,0:T(8,128)(2,1)S(1)}, bf16[128,1024]{1,0:T(8,128)(2,1)S(1)}, u32[]{:S(2)}, u32[]{:S(2)}) collective-permute-start(bf16[128,1024]{1,0:T(8,128)(2,1)S(1)} %get-tuple-element.13), channel_id=1, source_target_pairs={{0,1},{1,2},{2,3},{3,4},{4,5},{5,6},{6,7},{7,8},{8,9},{9,10},{10,1... | collective-permute-start | bytes 786440 | tf_op jit(solution)/shard_map/ppermute | solution.py:25
  19.5 19.7 %collective-permute-start.1 = (bf16[128,1024]{1,0:T(8,128)(2,1)S(1)}, bf16[128,1024]{1,0:T(8,128)(2,1)S(1)}, u32[]{:S(2)}, u32[]{:S(2)}) collective-permute-start(bf16[128,1024]{1,0:T(8,128)(2,1)S(1)} %get-tuple-element.14), channel_id=1, source_target_pairs={{1,0},{2,1},{3,2},{4,3},{5,4},{6,5},{7,6},{8,7},{9,8},{10,9},{11,1... | collective-permute-start | bytes 786440 | tf_op jit(solution)/shard_map/ppermute | solution.py:28
  27.3 11.7 %copy-start.24 = (s32[8,256]{1,0:T(8,128)S(1)}, s32[8,256]{1,0:T(8,128)}, u32[]{:S(2)}) copy-start(s32[8,256]{1,0:T(8,128)} %param.23) | copy-start | bytes 24580
  27.3 11.8 %copy-start.22 = (s32[3,1024]{1,0:T(4,128)S(1)}, s32[3,1024]{1,0:T(4,128)}, u32[]{:S(2)}) copy-start(s32[3,1024]{1,0:T(4,128)} %param.25) | copy-start | bytes 36868
  27.3 11.9 %copy-start.23 = (f32[3,1024]{1,0:T(4,128)S(1)}, f32[3,1024]{1,0:T(4,128)}, u32[]{:S(2)}) copy-start(f32[3,1024]{1,0:T(4,128)} %param.26) | copy-start | bytes 36868
  27.3 230.5 %all-to-all-start = ((bf16[64,16,1024]{2,1,0:T(8,128)(2,1)}), bf16[64,16,1024]{2,1,0:T(8,128)(2,1)}, u32[]{:S(2)}, u32[]{:S(2)}) async-start(bf16[64,16,1024]{2,1,0:T(8,128)(2,1)} %broadcast_in_dim.7), calls=%async_computation | async-start | bytes 4194304 | tf_op jit(solution)/shard_map/all_to_all | solution.py:44
  39.2 138.4 %copy-start.26 = (bf16[128,1024]{1,0:T(8,128)(2,1)}, bf16[128,1024]{1,0:T(8,128)(2,1)S(1)}, u32[]{:S(2)}) copy-start(bf16[128,1024]{1,0:T(8,128)(2,1)S(1)} %collective-permute-done) | copy-start | bytes 786436
  39.2 138.3 %copy-start.27 = (bf16[128,1024]{1,0:T(8,128)(2,1)}, bf16[128,1024]{1,0:T(8,128)(2,1)S(1)}, u32[]{:S(2)}) copy-start(bf16[128,1024]{1,0:T(8,128)(2,1)S(1)} %collective-permute-done.1) | copy-start | bytes 786436
  212.3 2.5 copy-start.13
  212.3 2.5 copy-start.14
  212.3 2.5 copy-start.15
  212.4 2.5 copy-start.16
  212.4 2.5 copy-start.17
  212.4 2.5 copy-start.18
  212.4 2.6 copy-start.19
  212.4 2.8 copy-start.20
  233.8 2.7 copy-start.10
  236.7 3.5 copy-start.11
  241.4 4.5 %copy-start.12 = (bf16[256,1024]{1,0:T(8,128)(2,1)S(1)}, bf16[256,1024]{1,0:T(8,128)(2,1)}, u32[]{:S(2)}) copy-start(bf16[256,1024]{1,0:T(8,128)(2,1)} %gather_fusion.2) | copy-start | bytes 1572868
  249.4 3.9 %copy-start.9 = (f32[256,1024]{0,1:T(8,128)S(1)}, f32[256,1024]{0,1:T(8,128)}, u32[]{:S(2)}) copy-start(f32[256,1024]{0,1:T(8,128)} %copy.104) | copy-start | bytes 3145732
  249.4 5.5 %copy-start.8 = (f32[256,1024]{0,1:T(8,128)S(1)}, f32[256,1024]{0,1:T(8,128)}, u32[]{:S(2)}) copy-start(f32[256,1024]{0,1:T(8,128)} %copy.92) | copy-start | bytes 3145732
  251.4 5.1 %copy-start.6 = (f32[256,1024]{0,1:T(8,128)S(1)}, f32[256,1024]{0,1:T(8,128)}, u32[]{:S(2)}) copy-start(f32[256,1024]{0,1:T(8,128)} %copy.93) | copy-start | bytes 3145732
  251.4 5.1 %copy-start.7 = (f32[256,1024]{0,1:T(8,128)S(1)}, f32[256,1024]{0,1:T(8,128)}, u32[]{:S(2)}) copy-start(f32[256,1024]{0,1:T(8,128)} %copy.95) | copy-start | bytes 3145732
  253.3 3.2 copy-start.2
  253.3 3.2 copy-start.3
  253.3 3.2 copy-start.4
  253.3 3.2 copy-start.5
  283.5 18.1 %all-to-all-start.1 = ((bf16[8,2,6400]{2,1,0:T(2,128)(2,1)}), bf16[8,2,6400]{2,1,0:T(2,128)(2,1)S(1)}, u32[]{:S(2)}, u32[]{:S(2)}) async-start(bf16[8,2,6400]{2,1,0:T(2,128)(2,1)} %reshape.717), calls=%async_computation.1 | async-start | bytes 409600 | tf_op jit(solution)/shard_map/all_to_all | solution.py:153
  308.0 59.0 %all-to-all-start.2 = ((bf16[8,100,128]{2,1,0:T(8,128)(2,1)}), bf16[8,100,128]{2,1,0:T(8,128)(2,1)S(1)}, u32[]{:S(2)}, u32[]{:S(2)}) async-start(bf16[8,100,128]{2,1,0:T(8,128)(2,1)} %copy.110), calls=%async_computation.2 | async-start | bytes 425984 | tf_op jit(solution)/shard_map/all_to_all | solution.py:174
Sparse Core Ops, SparseCore 0:
  10.7 163.9 all-gather.1
where the time goes:
time: 377 us; the launch traced here: 376 us
  waiting for transfers between devices  144 us (38%)
  local copies, waits for them, and re-layouts  88.6 us (24%)
  blocking collectives  54.3 us (14%)
  starting transfers between devices  34 us (9%)
  other arithmetic  22.9 us (6%)
  between operations  16.6 us (4%)
  matrix products  15.6 us (4%)
    all_gather x1, waiting for transfers between devices, in_one_piece(): lax.all_gather(both, axis, axis=dim, tiled=True)  135 us
    psum x5, blocking collectives, by_axis(): return functools.reduce(lax.psum, axes, shard)  54.3 us
    mul x8, local copies, waits for them, and re-layouts, attention(): weight = jnp.exp(jnp.sum(query_wide * gathered_key, axis=2) * factor)  18 us
    gather x8, local copies, waits for them, and re-layouts, attention(): value_ext[picked].astype(jnp.float32).reshape(row_count, HEADS, head_size)  15.9 us
    gather x8, local copies, waits for them, and re-layouts, attention(): key_ext[picked].astype(jnp.float32).reshape(row_count, HEADS, head_size)  15.8 us
    gather x3, local copies, waits for them, and re-layouts, decode(): processed[sources[neighbour]].astype(jnp.float32)  14.8 us
    convert_element_type x8, local copies, waits for them, and re-layouts, attention(): value_ext[picked].astype(jnp.float32).reshape(row_count, HEADS, head_size)  12.9 us
    all_to_all x1, starting transfers between devices, from_everyone(): return lax.all_to_all(copies, axis, split_axis=0, concat_axis=0, tiled=True)  11.6 us
  transfers between devices with their start and end apart: 6, of which 2 were waited for; matrix products, arithmetic and copies ran while one was open for 25% of the time, Pallas kernels for 0%

commit v1 on v0

v1 whole, which is shorter than its diff:
```python
import functools

import jax
import jax.numpy as jnp
from jax import lax
from jax.experimental import pallas as pl
from jax.experimental.pallas import tpu as pltpu
from jax.sharding import Mesh
from jax.sharding import PartitionSpec as P

SPACE = ("space_0", "space_1", "space_2")
MEMBER = ("member_0", "member_1")
SMOOTH2 = 0.0625
EPS = 1e-05
F32 = jnp.float32
BF16 = jnp.bfloat16
NEG = -1e30
VMEM = pl.BlockSpec(memory_space=pltpu.VMEM)

OFFSETS = (1, 7, 2, 6, 3, 5, 4)


def dot(a, b, ca, cb):
    return lax.dot_general(a, b, (((ca,), (cb,)), ((), ())), preferred_element_type=F32)


def place():
    return tuple(lax.axis_index(a) for a in MEMBER + SPACE)


def remote(src, dst, send, recv, device):
    return pltpu.make_async_remote_copy(
        src_ref=src,
        dst_ref=dst,
        send_sem=send,
        recv_sem=recv,
        device_id=device,
        device_id_type=pl.DeviceIdType.MESH,
    )


def at_y(me, step):
    yh, x, z, yl, c = me
    y = lax.rem(4 * yh + yl + 8 + step, 8)
    return (y // 4, x, z, lax.rem(y, 4), c)


def at_z(me, step):
    yh, x, z, yl, c = me
    return (yh, x, lax.rem(z + 8 + step, 8), yl, c)


def at_x(me, step):
    yh, x, z, yl, c = me
    return (yh, lax.rem(x + 4 + step, 4), z, yl, c)


def at_core(me):
    yh, x, z, yl, c = me
    return (yh, x, z, yl, 1 - c)


def at_block(me, step):
    yh, x, z, yl, c = me
    s = lax.rem(z * 8 + yl * 2 + c + 64 + step, 64)
    return (yh, x, s // 8, lax.rem(s, 8) // 2, lax.rem(s, 2))


def greet(devices):
    barrier = pltpu.get_barrier_semaphore()
    for d in devices:
        pl.semaphore_signal(barrier, inc=1, device_id=d, device_id_type=pl.DeviceIdType.MESH)
    return lambda: pl.semaphore_wait(barrier, len(devices))


def gather_kernel(
    wq, wk, wv, wo, wd, states, noise, rows,
    wall, halo, nhalo, nown,
    picked, npicked,
    zs, zr, ys, yr, cs, cr, hs, hr, ns, nr, xs, xr,
):
    me = place()
    yh, x, z, yl, c = me
    wait_all = greet(
        [at_z(me, o) for o in OFFSETS]
        + [at_y(me, 1), at_y(me, -1), at_y(me, 2), at_y(me, -2), at_core(me)]
        + [at_x(me, 1), at_x(me, 2), at_x(me, 3)]
        + [at_block(me, 1), at_block(me, -1)]
    )
    columns = pl.ds(pl.multiple_of(256 * x, 256), 256)
    mine = wall.at[z, yl, c]
    mine[:, 0:256] = wq[:, columns]
    mine[:, 256:512] = wk[:, columns]
    mine[:, 512:768] = wv[:, columns]
    mine[:, 768:896] = dot(wo[...], wd[...], 1, 1).astype(BF16)
    nown[x] = noise[...]
    chosen = (lax.broadcasted_iota(jnp.int32, (256, 256), 0) == rows[...]).astype(F32).astype(BF16)
    picked[...] = dot(chosen, states[...], 0, 0).astype(BF16).reshape(2, 128, 1024)
    sent_noise = dot(noise[...], chosen, 1, 0).astype(BF16)
    npicked[0] = sent_noise[:, 0:128]
    npicked[1] = sent_noise[:, 128:256]
    wait_all()

    started = []

    def go(copy):
        copy.start()
        started.append(copy)

    quarter = pl.ds(pl.multiple_of(32 * x, 32), 32)
    for i, (half, step) in enumerate(((1, 1), (0, -1))):
        go(remote(picked.at[half, quarter], halo.at[i, quarter], hs.at[i], hr.at[i], at_block(me, step)))
        go(remote(npicked.at[half], nhalo.at[x, i], ns.at[i], nr.at[i], at_block(me, step)))
    for o in OFFSETS:
        go(remote(mine, mine, zs.at[o], zr.at[o], at_z(me, o)))
    for t in (1, 2, 3):
        go(remote(nown.at[x], nown.at[x], xs.at[t, 0], xr.at[t, 0], at_x(me, t)))

    def y_steps(k):
        return (1, -1, 2 if k % 2 == 0 else -2)

    def forward_y(k, o):
        zk = lax.rem(z + 8 - o, 8)
        for t, step in enumerate(y_steps(k)):
            block = wall.at[zk, yl, c]
            go(remote(block, block, ys.at[k, t], yr.at[k, t], at_y(me, step)))

    def forward_core(k, o):
        zk = lax.rem(z + 8 - o, 8)
        for t, step in enumerate(y_steps(k)):
            landed = wall.at[zk, lax.rem(yl + 4 - step, 4), c]
            remote(landed, landed, ys.at[k, t], yr.at[k, t], at_y(me, -step)).wait_recv()
        both = wall.at[zk, :, c]
        go(remote(both, both, cs.at[k], cr.at[k], at_core(me)))

    def forward_x():
        for i, step in enumerate((1, -1)):
            part = halo.at[i, quarter]
            remote(part, part, hs.at[i], hr.at[i], at_block(me, -step)).wait_recv()
            part = nhalo.at[x, i]
            remote(part, part, ns.at[i], nr.at[i], at_block(me, -step)).wait_recv()
        for t in (1, 2, 3):
            go(remote(halo.at[:, quarter], halo.at[:, quarter], xs.at[t, 1], xr.at[t, 1], at_x(me, t)))
            go(remote(nhalo.at[x], nhalo.at[x], xs.at[t, 2], xr.at[t, 2], at_x(me, t)))

    order = (0,) + OFFSETS
    for k, o in enumerate(order):
        if o:
            landed = wall.at[lax.rem(z + 8 - o, 8), yl, c]
            remote(landed, landed, zs.at[o], zr.at[o], at_z(me, -o)).wait_recv()
        forward_y(k, o)
        if k == 3:
            forward_x()
        if k >= 2:
            forward_core(k - 2, order[k - 2])
    forward_core(6, order[6])
    forward_core(7, order[7])
    for k, o in enumerate(order):
        landed = wall.at[lax.rem(z + 8 - o, 8), :, 1 - c]
        remote(landed, landed, cs.at[k], cr.at[k], at_core(me)).wait_recv()
    for t in (1, 2, 3):
        other = lax.rem(x + 4 - t, 4)
        slot = nown.at[other]
        remote(slot, slot, xs.at[t, 0], xr.at[t, 0], at_x(me, -t)).wait_recv()
        slot = halo.at[:, pl.ds(pl.multiple_of(32 * other, 32), 32)]
        remote(slot, slot, xs.at[t, 1], xr.at[t, 1], at_x(me, -t)).wait_recv()
        slot = nhalo.at[other]
        remote(slot, slot, xs.at[t, 2], xr.at[t, 2], at_x(me, -t)).wait_recv()
    for copy in started:
        copy.wait_send()


def attend_kernel(
    wall, states, halo, nown, nhalo, gain, cond, edges,
    out,
    normed, counts, hidden, wvt, w2t, att,
):
    x = lax.axis_index(MEMBER[1])

    def normalise(values, at):
        v = values.astype(F32)
        center = v - jnp.mean(v, axis=1, keepdims=True)
        spread = jnp.mean(center * center, axis=1, keepdims=True)
        normed[pl.ds(at, 128), :] = center * lax.rsqrt(spread + EPS) * gain[...]

    normalise(halo[0], 0)
    normalise(states[0:128, :], 128)
    normalise(states[128:256, :], 256)
    normalise(halo[1], 384)
    row = lax.broadcasted_iota(jnp.int32, (512, 256), 0)
    total = jnp.zeros((512, 256), F32)
    for k in range(8):
        total = total + (row == edges[k : k + 1, :]).astype(F32)
    counts[...] = total
    weights = wall[...].reshape(1024, 896)
    wvt[...] = weights[:, 512:768].T
    pair = wall[pl.ds(2 * x, 2)].reshape(256, 896)
    w2t[...] = pair[:, 768:896].T
    lane = lax.broadcasted_iota(jnp.int32, (256, 256), 1) // 64

    def member(m, _):
        noises = (nhalo[m, 0], nown[m, :, 0:128], nown[m, :, 128:256], nhalo[m, 1])
        for i in range(4):
            terms = dot(noises[i], cond[...], 0, 0)
            rows = slice(128 * i, 128 * i + 128)
            hidden[rows, :] = (normed[rows, :] * (1.0 + terms[:, :1024]) + terms[:, 1024:]).astype(BF16)
        all_rows = hidden[...]
        w = wall[...].reshape(1024, 896)
        query = dot(hidden[128:384, :], w[:, 0:256], 1, 0).astype(BF16) * 0.125
        key = dot(all_rows, w[:, 256:512], 1, 0).astype(BF16)
        value_t = dot(wvt[...], all_rows, 1, 1).astype(BF16)
        for h in range(4):
            one = jnp.where(lane == h, query, jnp.zeros_like(query))
            scores = dot(key, one, 1, 1)
            count = counts[...]
            scores = jnp.where(count > 0.0, scores, NEG)
            top = jnp.max(scores, axis=0, keepdims=True)
            weight = jnp.exp(scores - top) * count
            below = jnp.sum(weight, axis=0, keepdims=True)
            above = dot(value_t[64 * h : 64 * h + 64, :], weight.astype(BF16), 1, 0)
            att[64 * h : 64 * h + 64, :] = (above / below).astype(BF16)
        out[m] = dot(w2t[...], att[...], 1, 0).astype(BF16)
        return 0

    lax.fori_loop(0, 4, member, 0)


def score_kernel(
    part, states, wd, dec_src, dec_weight, truth, area,
    grad, loss,
    got, mine, theirs, wide, tall, fields, made, l0, l1, l2, l3, b1, b2, b3,
    ps, pr, ys, yr, gs, gr, ls, lr,
):
    me = place()
    yh, x, z, yl, c = me
    plane = [
        (yh, lax.rem(x + dx, 4), z, yl, lax.rem(c + dc, 2))
        for dx in range(4)
        for dc in range(2)
        if dx or dc
    ]
    plane_from = [
        (yh, lax.rem(x + 4 - dx, 4), z, yl, lax.rem(c + dc, 2))
        for dx in range(4)
        for dc in range(2)
        if dx or dc
    ]
    wait_all = greet(
        plane + [at_z(me, o) for o in range(1, 8)] + [at_y(me, o) for o in range(1, 8)]
    )
    node = lax.broadcasted_iota(jnp.int32, (256, 1024), 0)
    select = jnp.zeros((256, 1024), F32)
    for k in range(3):
        select = select + jnp.where(node == dec_src[k : k + 1, :], dec_weight[k : k + 1, :], 0.0)
    wide[0] = select.astype(BF16)
    wide[1] = (select - wide[0].astype(F32)).astype(BF16)
    tall[...] = jnp.zeros_like(tall)
    tall[0:100, :] = truth[...].astype(F32)
    group = pl.ds(pl.multiple_of(32 * x, 32), 32)
    base = dot(wd[group, :], states[...], 1, 1)
    wait_all()

    started = []

    def go(copy):
        copy.start()
        started.append(copy)

    for t in (1, 2, 3):
        peer = at_x(me, t)
        rows = pl.ds(pl.multiple_of(32 * peer[1], 32), 32)
        go(remote(part.at[:, rows], got.at[t], ps.at[t], pr.at[t], peer))
    update = part[:, group, :].astype(F32)
    for t in (1, 2, 3):
        remote(got.at[t], got.at[t], ps.at[t], pr.at[t], at_x(me, -t)).wait_recv()
        update = update + got[t].astype(F32)
    mine[...] = update.astype(BF16)
    go(remote(mine, theirs, ys.at[0], yr.at[0], at_y(me, 4)))

    def decode(source, at):
        for m in range(4):
            whole = base + source[m].astype(F32)
            high = whole.astype(BF16)
            low = (whole - high.astype(F32)).astype(BF16)
            value = dot(high, wide[0], 1, 0) + dot(low, wide[0], 1, 0) + dot(high, wide[1], 1, 0)
            fields[at + m] = value.astype(BF16).astype(F32)

    decode(mine, 0)
    remote(theirs, theirs, ys.at[0], yr.at[0], at_y(me, 4)).wait_recv()
    decode(theirs, 4)

    valid = lax.broadcasted_iota(jnp.int32, (32, 128), 0) + 32 * x < 100

    def columns(i, carry):
        cols = pl.ds(pl.multiple_of(128 * i, 128), 128)
        a = area[:, cols]
        y = tall[group, cols]
        f = [fields[m, :, cols] for m in range(8)]
        slopes = [jnp.zeros((32, 128), F32) for _ in range(4)]
        spread = jnp.zeros((32, 128), F32)
        skill = jnp.zeros((32, 128), F32)
        for m in range(4):
            for n in range(m + 1, 8):
                d = f[m] - f[n]
                q = d * d + SMOOTH2
                r = lax.rsqrt(q)
                s = d * r
                slopes[m] = slopes[m] + s
                if n < 4:
                    slopes[n] = slopes[n] - s
                    spread = spread + 2.0 * (q * r)
                else:
                    spread = spread + q * r
        for m in range(4):
            d = f[m] - y
            q = d * d + SMOOTH2
            r = lax.rsqrt(q)
            skill = skill + q * r
            made[m, :, cols] = (a * (d * r - slopes[m] * (1.0 / 7.0))).astype(BF16)
        score = a * (skill * (1.0 / 8.0) - spread * (1.0 / 112.0))
        score = jnp.where(valid, score, 0.0)
        return carry + score

    total = lax.fori_loop(0, 8, columns, jnp.zeros((32, 128), F32))
    l0[...] = total[0:8] + total[8:16] + total[16:24] + total[24:32]

    for t, peer in enumerate(plane):
        go(remote(l0, b1.at[t], ls.at[0, t], lr.at[0, t], peer))
    for t in (1, 2, 3):
        peer = at_x(me, t)
        go(remote(made.at[peer[1]], grad.at[group], gs.at[t], gr.at[t], peer))
    grad[group, :] = made[x]

    def collect(here, inbox, stage, sources):
        value = here[...]
        for t, peer in enumerate(sources):
            remote(inbox.at[t], inbox.at[t], ls.at[stage, t], lr.at[stage, t], peer).wait_recv()
            value = value + inbox[t]
        return value

    l1[...] = collect(l0, b1, 0, plane_from)
    for t in range(7):
        go(remote(l1, b2.at[t], ls.at[1, t], lr.at[1, t], at_z(me, t + 1)))
    l2[...] = collect(l1, b2, 1, [at_z(me, -t) for t in range(1, 8)])
    for t in range(7):
        go(remote(l2, b3.at[t], ls.at[2, t], lr.at[2, t], at_y(me, t + 1)))
    value = collect(l2, b3, 2, [at_y(me, -t) for t in range(1, 8)])
    value = jnp.sum(jnp.sum(value, axis=0, keepdims=True), axis=1, keepdims=True)
    loss[...] = value * (1.0 / 6553600.0)
    for t in (1, 2, 3):
        peer = at_x(me, -t)
        rows = pl.ds(pl.multiple_of(32 * peer[1], 32), 32)
        remote(grad.at[rows], grad.at[rows], gs.at[t], gr.at[t], peer).wait_recv()
    for copy in started:
        copy.wait_send()


def dma(*shape):
    return pltpu.SemaphoreType.DMA(shape)


def per_device(
    node_states, noise, norm_gain, cond_weight, w_query, w_key, w_value, w_out,
    edge_src, send_rows, dec_src, dec_weight, w_decode, truth, area,
):
    decoder = jnp.pad(w_decode, ((0, 28), (0, 0)))
    wall, halo, nhalo, nown = pl.pallas_call(
        gather_kernel,
        out_shape=(
            jax.ShapeDtypeStruct((8, 4, 2, 16, 896), BF16),
            jax.ShapeDtypeStruct((2, 128, 1024), BF16),
            jax.ShapeDtypeStruct((4, 2, 16, 128), BF16),
            jax.ShapeDtypeStruct((4, 16, 256), BF16),
        ),
        in_specs=[VMEM] * 8,
        out_specs=(VMEM,) * 4,
        scratch_shapes=[
            pltpu.VMEM((2, 128, 1024), BF16),
            pltpu.VMEM((2, 16, 128), BF16),
            dma(8), dma(8), dma(8, 3), dma(8, 3), dma(8), dma(8), dma(2), dma(2), dma(2), dma(2),
            dma(4, 3), dma(4, 3),
        ],
        compiler_params=pltpu.CompilerParams(collective_id=0, has_side_effects=True),
        name="gather",
    )(w_query, w_key, w_value, w_out, decoder, node_states, noise[0], send_rows.reshape(1, 256))
    part = pl.pallas_call(
        attend_kernel,
        out_shape=jax.ShapeDtypeStruct((4, 128, 256), BF16),
        in_specs=[VMEM] * 8,
        out_specs=VMEM,
        scratch_shapes=[
            pltpu.VMEM((512, 1024), F32),
            pltpu.VMEM((512, 256), F32),
            pltpu.VMEM((512, 1024), BF16),
            pltpu.VMEM((256, 1024), BF16),
            pltpu.VMEM((128, 256), BF16),
            pltpu.VMEM((256, 256), BF16),
        ],
        compiler_params=pltpu.CompilerParams(vmem_limit_bytes=48 * 1024 * 1024),
        name="attend",
    )(wall, node_states, halo, nown, nhalo, norm_gain.reshape(1, 1024), cond_weight, edge_src)
    grad, loss = pl.pallas_call(
        score_kernel,
        out_shape=(
            jax.ShapeDtypeStruct((128, 1024), BF16),
            jax.ShapeDtypeStruct((1, 1), F32),
        ),
        in_specs=[VMEM] * 7,
        out_specs=(VMEM, VMEM),
        scratch_shapes=[
            pltpu.VMEM((4, 4, 32, 256), BF16),
            pltpu.VMEM((4, 32, 256), BF16),
            pltpu.VMEM((4, 32, 256), BF16),
            pltpu.VMEM((2, 256, 1024), BF16),
            pltpu.VMEM((128, 1024), F32),
            pltpu.VMEM((8, 32, 1024), F32),
            pltpu.VMEM((4, 32, 1024), BF16),
            pltpu.VMEM((8, 128), F32),
            pltpu.VMEM((8, 128), F32),
            pltpu.VMEM((8, 128), F32),
            pltpu.VMEM((8, 128), F32),
            pltpu.VMEM((7, 8, 128), F32),
            pltpu.VMEM((7, 8, 128), F32),
            pltpu.VMEM((7, 8, 128), F32),
            dma(4), dma(4), dma(1), dma(1), dma(4), dma(4), dma(3, 7), dma(3, 7),
        ],
        compiler_params=pltpu.CompilerParams(collective_id=1, has_side_effects=True),
        name="score",
    )(part, node_states, decoder, dec_src, dec_weight, truth, area.reshape(1, 1024))
    return loss[0, 0], grad[None, :100]


def solution(mesh):
    split = Mesh(mesh.devices.reshape(2, 4, 8, 4, 2), MEMBER + SPACE)
    return jax.shard_map(
        per_device,
        mesh=split,
        in_specs=(
            P(SPACE, None),
            P(MEMBER, None, SPACE),
            P(),
            P(),
            P(SPACE, None),
            P(SPACE, None),
            P(SPACE, None),
            P(SPACE, None),
            P(None, SPACE),
            P(SPACE),
            P(None, SPACE),
            P(None, SPACE),
            P(),
            P(None, SPACE),
            P(SPACE),
        ),
        out_specs=(P(), P(MEMBER, None, SPACE)),
        check_vma=False,
    )
```

time: 377 us -> 98.8 us (0.26)
  waiting for transfers between devices: 144 us -> 0 us
  Pallas kernels: 0 us -> 84.1 us
  local copies, waits for them, and re-layouts: 88.6 us -> 11.3 us
  blocking collectives: 54.3 us -> 0 us
  starting transfers between devices: 34 us -> 0 us
  other arithmetic: 22.9 us -> 0 us
  matrix products: 15.6 us -> 0 us
  between operations: 16.6 us -> 2.38 us
    all_gather x1 -> x0, waiting for transfers between devices: 135 us -> none  [in_one_piece(): lax.all_gather(both, axis, axis=dim, tiled=True)]
    pallas_call x0 -> x3, Pallas kernels: none -> 84.1 us  [the longest x1 36.2 us: per_device(): pl.pallas_call(gather_kernel, out_shape=(jax.ShapeDtypeStruct((8, 4, 2, 1...]
    psum x5 -> x0, blocking collectives: 54.3 us -> none  [by_axis(): return functools.reduce(lax.psum, axes, shard)]
    gather x20 -> x0, local copies, waits for them, and re-layouts: 47.7 us -> none  [the longest x8 15.9 us: attention(): value_ext[picked].astype(jnp.float32).reshape(row_count, HEADS, head_size)]
    all_to_all x3 -> x0, starting transfers between devices: 23.3 us -> none  [the longest x1 11.6 us: from_everyone(): return lax.all_to_all(copies, axis, split_axis=0, concat_axis=0, tiled=True)]
    mul x8 -> x0, local copies, waits for them, and re-layouts: 18 us -> none  [attention(): weight = jnp.exp(jnp.sum(query_wide * gathered_key, axis=2) * factor)]
    dot_general x6 -> x0, matrix products: 15.6 us -> none  [the longest x1 3.67 us: decode(): lax.dot_general(w_decode, gathered.astype(jnp.bfloat16), (((1,), (1,)), (...]
    convert_element_type x9 -> x0, local copies, waits for them, and re-layouts: 13.6 us -> none  [the longest x8 12.9 us: attention(): value_ext[picked].astype(jnp.float32).reshape(row_count, HEADS, head_size)]
  transfers between devices with their start and end apart: 6 -> 0, of which waited for: 2 -> 0; matrix products, arithmetic and copies ran while one was open for 25% -> 0% of each run, Pallas kernels for 0% -> 0%
where the time goes in v1:
time: 98.8 us; the launch traced here: 97.8 us
  Pallas kernels  84.1 us (85%)
  local copies, waits for them, and re-layouts  11.3 us (11%)
  between operations  2.38 us (2%)
    pallas_call x1, Pallas kernels, per_device(): pl.pallas_call(gather_kernel, out_shape=(jax.ShapeDtypeStruct((8, 4, 2, 1...  36.2 us
    pallas_call x1, Pallas kernels, per_device(): pl.pallas_call(score_kernel, out_shape=(jax.ShapeDtypeStruct((128, 1024),...  33 us
    pallas_call x1, Pallas kernels, per_device(): pl.pallas_call(attend_kernel, out_shape=jax.ShapeDtypeStruct((4, 128, 256...  14.9 us
    unnamed x18, local copies, waits for them, and re-layouts  8.02 us

profile of v1, /device:TPU:1, one launch (start us, length us, event | category | flops | bytes accessed | tf_op | source)
XLA Modules:
  0.0 97.8 jit_solution(16777634365450868880)
XLA Ops:
  0.6 1.7 %pad.4.wd = bf16[128,1024]{1,0:T(8,128)(2,1)} pad(bf16[100,1024]{1,0:T(8,128)(2,1)} %param.27, bf16[]{:T(256)} %constant.2.clone.1), padding=0_28x0_0 | pad | bytes 466946 | tf_op jit(solution)/shard_map/jit(_pad)/pad | solution.py:366
  2.3 36.2 %gather.1 = (bf16[8,4,2,16,896]{4,3,2,1,0:T(8,128)(2,1)}, bf16[2,128,1024]{2,1,0:T(8,128)(2,1)}, bf16[4,2,16,128]{3,2,1,0:T(8,128)(2,1)}, bf16[4,16,256]{2,1,0:T(8,128)(2,1)}) custom-call(bf16[16,1024]{1,0:T(8,128)(2,1)} %wq.1, bf16[16,1024]{1,0:T(8,128)(2,1)} %wk.1, bf16[16,1024]{1,0:T(8,128)(2,1)} %wv.1, bf16[16,1024]{1,0:T(8,128)(2,1)} %wo.1, ...), custom_call_target="tpu_custom_call" | custom-call | tf_op jit(solution)/shard_map/gather/pallas_call | solution.py:367
  38.5 0.0 copy-start
  38.5 1.0 %copy-done = bf16[256,1024]{1,0:T(8,128)(2,1)S(1)} copy-done((bf16[256,1024]{1,0:T(8,128)(2,1)S(1)}, bf16[256,1024]{1,0:T(8,128)(2,1)}, u32[]{:S(2)}) %copy-start) | copy-done | bytes 524312
  39.5 0.0 copy-start.1
  39.5 1.5 %copy-done.1 = bf16[8,4,2,16,896]{4,3,2,1,0:T(8,128)(2,1)S(1)} copy-done((bf16[8,4,2,16,896]{4,3,2,1,0:T(8,128)(2,1)S(1)}, bf16[8,4,2,16,896]{4,3,2,1,0:T(8,128)(2,1)}, u32[]{:S(2)}) %copy-start.1) | copy-done | bytes 1835032
  41.0 0.0 copy-start.3
  41.0 1.0 %copy-done.3 = bf16[2,128,1024]{2,1,0:T(8,128)(2,1)S(1)} copy-done((bf16[2,128,1024]{2,1,0:T(8,128)(2,1)S(1)}, bf16[2,128,1024]{2,1,0:T(8,128)(2,1)}, u32[]{:S(2)}) %copy-start.3) | copy-done | bytes 524312
  42.1 0.0 copy-start.4
  42.1 0.8 copy-done.4
  42.9 0.0 copy-start.5
  42.9 0.8 copy-done.5
  43.7 0.0 copy-start.6
  43.7 0.8 copy-done.6
  44.4 0.0 copy-start.7
  44.4 0.7 copy-done.7
  45.1 0.0 copy-start.8
  45.1 0.7 copy-done.8
  45.8 14.9 %attend.1.part = bf16[4,128,256]{2,1,0:T(8,128)(2,1)S(1)} custom-call(bf16[8,4,2,16,896]{4,3,2,1,0:T(8,128)(2,1)S(1)} %copy-done.1, bf16[256,1024]{1,0:T(8,128)(2,1)S(1)} %copy-done, bf16[2,128,1024]{2,1,0:T(8,128)(2,1)S(1)} %copy-done.3, bf16[4,16,256]{2,1,0:T(8,128)(2,1)S(1)} %copy-done.6, bf16[4,2,16,128]{3,2,1,0:T(8,128)(2,1)S(1)} %copy-done.5, ...), custom_call_target="tpu_custom_call" | custom-call | tf_op jit(solution)/shard_map/attend/pallas_call | solution.py:386
  60.7 0.0 copy-start.2
  60.8 0.7 copy-done.2
  61.5 33.0 %score.1 = (bf16[128,1024]{1,0:T(8,128)(2,1)}, f32[1,1]{1,0:T(1,128)}) custom-call(bf16[4,128,256]{2,1,0:T(8,128)(2,1)} %copy-done.2, bf16[256,1024]{1,0:T(8,128)(2,1)} %states.5, bf16[128,1024]{1,0:T(8,128)(2,1)} %pad.4.wd, s32[3,1024]{1,0:T(4,128)} %dec_src.1, f32[3,1024]{1,0:T(4,128)} %dec_weight.1, bf16[100,1024]{1,0:T(8,128)(2,1)} %truth.1, ...), custom_call_target="tpu_custom_call" | custom-call | tf_op jit(solution)/shard_map/score/pallas_call | solution.py:402
  94.4 1.6 %slice_bitcast_fusion = bf16[1,100,1024]{2,1,0:T(8,128)(2,1)} fusion(bf16[128,1024]{1,0:T(8,128)(2,1)} %get-tuple-element.13), kind=kLoop, calls=%fused_computation | loop fusion | bytes 409600 | tf_op jit(solution)/shard_map/broadcast_in_dim | solution.py:430
Async XLA Ops:
  38.5 1.0 %copy-start = (bf16[256,1024]{1,0:T(8,128)(2,1)S(1)}, bf16[256,1024]{1,0:T(8,128)(2,1)}, u32[]{:S(2)}) copy-start(bf16[256,1024]{1,0:T(8,128)(2,1)} %states.5) | copy-start | bytes 1572868
  39.5 1.5 %copy-start.1 = (bf16[8,4,2,16,896]{4,3,2,1,0:T(8,128)(2,1)S(1)}, bf16[8,4,2,16,896]{4,3,2,1,0:T(8,128)(2,1)}, u32[]{:S(2)}) copy-start(bf16[8,4,2,16,896]{4,3,2,1,0:T(8,128)(2,1)} %get-tuple-element.8.wall) | copy-start | bytes 5505028
  41.0 1.0 %copy-start.3 = (bf16[2,128,1024]{2,1,0:T(8,128)(2,1)S(1)}, bf16[2,128,1024]{2,1,0:T(8,128)(2,1)}, u32[]{:S(2)}) copy-start(bf16[2,128,1024]{2,1,0:T(8,128)(2,1)} %get-tuple-element.9.halo) | copy-start | bytes 1572868
  42.1 0.8 copy-start.4
  42.9 0.8 copy-start.5
  43.7 0.8 copy-start.6
  44.4 0.7 copy-start.7
  45.1 0.7 copy-start.8
  60.7 0.7 copy-start.2

commit v2 on v1

v2 whole, which is shorter than its diff:
```python
import functools

import jax
import jax.numpy as jnp
from jax import lax
from jax.experimental import pallas as pl
from jax.experimental.pallas import tpu as pltpu
from jax.sharding import Mesh
from jax.sharding import PartitionSpec as P

SPACE = ("space_0", "space_1", "space_2")
MEMBER = ("member_0", "member_1")
SMOOTH2 = 0.0625
EPS = 1e-05
F32 = jnp.float32
BF16 = jnp.bfloat16
NEG = -1e30
VMEM = pl.BlockSpec(memory_space=pltpu.VMEM)

OFFSETS = (1, 7, 2, 6, 3, 5, 4)


def dot(a, b, ca, cb):
    return lax.dot_general(a, b, (((ca,), (cb,)), ((), ())), preferred_element_type=F32)


def place():
    return tuple(lax.axis_index(a) for a in MEMBER + SPACE)


def remote(src, dst, send, recv, device):
    return pltpu.make_async_remote_copy(
        src_ref=src,
        dst_ref=dst,
        send_sem=send,
        recv_sem=recv,
        device_id=device,
        device_id_type=pl.DeviceIdType.MESH,
    )


def at_y(me, step):
    yh, x, z, yl, c = me
    y = lax.rem(4 * yh + yl + 8 + step, 8)
    return (y // 4, x, z, lax.rem(y, 4), c)


def at_z(me, step):
    yh, x, z, yl, c = me
    return (yh, x, lax.rem(z + 8 + step, 8), yl, c)


def at_x(me, step):
    yh, x, z, yl, c = me
    return (yh, lax.rem(x + 4 + step, 4), z, yl, c)


def at_core(me):
    yh, x, z, yl, c = me
    return (yh, x, z, yl, 1 - c)


def at_block(me, step):
    yh, x, z, yl, c = me
    s = lax.rem(z * 8 + yl * 2 + c + 64 + step, 64)
    return (yh, x, s // 8, lax.rem(s, 8) // 2, lax.rem(s, 2))


def greet(devices):
    barrier = pltpu.get_barrier_semaphore()
    for d in devices:
        pl.semaphore_signal(barrier, inc=1, device_id=d, device_id_type=pl.DeviceIdType.MESH)
    return lambda: pl.semaphore_wait(barrier, len(devices))


def step_kernel(
    wq, wk, wv, wo, states_in, noise_in, rows_in, gain_in, cond_in, edges_in, wd_in,
    source_in, weight_in, truth_in, area_in,
    grad, loss,
    states, noise, rows, gain, cond, edges, wd, source, weight, truth, area, wo_here,
    wall, halo, nhalo, nown, picked, npicked,
    normed, counts, hidden, wvt, w2t, att,
    part, got, mine, theirs, wide, tall, fields, slopes, scores, made, l0, l1, l2, b1, b2, b3,
    fetch, zs, zr, ys, yr, cs, cr, hs, hr, ns, nr, xs, xr, ps, pr, fs, fr, gs, gr, ls, lr,
):
    me = place()
    yh, x, z, yl, c = me
    plane = [
        (yh, lax.rem(x + dx, 4), z, yl, lax.rem(c + dc, 2))
        for dx in range(4)
        for dc in range(2)
        if dx or dc
    ]
    plane_from = [
        (yh, lax.rem(x + 4 - dx, 4), z, yl, lax.rem(c + dc, 2))
        for dx in range(4)
        for dc in range(2)
        if dx or dc
    ]
    wait_all = greet(
        [at_z(me, o) for o in OFFSETS]
        + [at_y(me, o) for o in range(1, 8)]
        + plane
        + [at_block(me, 1), at_block(me, -1)]
    )
    columns = pl.ds(pl.multiple_of(256 * x, 256), 256)
    own = wall.at[z, yl, c]
    fetches = [
        pltpu.make_async_copy(a, b, fetch.at[i])
        for i, (a, b) in enumerate(
            (
                (rows_in, rows),
                (states_in, states),
                (noise_in, noise),
                (noise_in, nown.at[x]),
                (wo, wo_here),
                (wd_in, wd),
                (wq.at[:, columns], own.at[:, 0:256]),
                (wk.at[:, columns], own.at[:, 256:512]),
                (wv.at[:, columns], own.at[:, 512:768]),
                (gain_in, gain),
                (cond_in, cond),
                (edges_in, edges),
                (source_in, source),
                (weight_in, weight),
                (truth_in, truth),
                (area_in, area),
            )
        )
    ]
    for f in fetches:
        f.start()
    for f in fetches[:3]:
        f.wait()
    chosen = (lax.broadcasted_iota(jnp.int32, (256, 256), 0) == rows[...]).astype(F32).astype(BF16)
    picked[...] = dot(chosen, states[...], 0, 0).astype(BF16).reshape(2, 128, 1024)
    sent_noise = dot(noise[...], chosen, 1, 0).astype(BF16)
    npicked[0] = sent_noise[:, 0:128]
    npicked[1] = sent_noise[:, 128:256]
    for f in fetches[3:9]:
        f.wait()
    wall[z, yl, c, :, 768:868] = dot(wo_here[...], wd[...], 1, 1).astype(BF16)
    wall[z, yl, c, :, 868:896] = jnp.zeros((16, 28), BF16)
    wait_all()

    started = []

    def go(copy):
        copy.start()
        started.append(copy)

    quarter = pl.ds(pl.multiple_of(32 * x, 32), 32)
    for i, (half, step) in enumerate(((1, 1), (0, -1))):
        go(remote(picked.at[half, quarter], halo.at[i, quarter], hs.at[i], hr.at[i], at_block(me, step)))
        go(remote(npicked.at[half], nhalo.at[x, i], ns.at[i], nr.at[i], at_block(me, step)))
    for o in OFFSETS:
        go(remote(own, own, zs.at[o], zr.at[o], at_z(me, o)))
    for t in (1, 2, 3):
        go(remote(nown.at[x], nown.at[x], xs.at[t, 0], xr.at[t, 0], at_x(me, t)))

    def y_steps(k):
        return (1, -1, 2 if k % 2 == 0 else -2)

    order = (0,) + OFFSETS

    def forward_y(k):
        zk = lax.rem(z + 8 - order[k], 8)
        block = wall.at[zk, yl, c]
        if k:
            remote(block, block, zs.at[order[k]], zr.at[order[k]], at_z(me, -order[k])).wait_recv()
        for t, step in enumerate(y_steps(k)):
            go(remote(block, block, ys.at[k, t], yr.at[k, t], at_y(me, step)))

    def forward_core(k):
        zk = lax.rem(z + 8 - order[k], 8)
        for t, step in enumerate(y_steps(k)):
            landed = wall.at[zk, lax.rem(yl + 4 - step, 4), c]
            remote(landed, landed, ys.at[k, t], yr.at[k, t], at_y(me, -step)).wait_recv()
        both = wall.at[zk, :, c]
        go(remote(both, both, cs.at[k], cr.at[k], at_core(me)))

    def forward_x():
        for i, step in enumerate((1, -1)):
            slot = halo.at[i, quarter]
            remote(slot, slot, hs.at[i], hr.at[i], at_block(me, -step)).wait_recv()
            slot = nhalo.at[x, i]
            remote(slot, slot, ns.at[i], nr.at[i], at_block(me, -step)).wait_recv()
        for t in (1, 2, 3):
            go(remote(halo.at[:, quarter], halo.at[:, quarter], xs.at[t, 1], xr.at[t, 1], at_x(me, t)))
            go(remote(nhalo.at[x], nhalo.at[x], xs.at[t, 2], xr.at[t, 2], at_x(me, t)))

    def normalise(values, at):
        v = values.astype(F32)
        center = v - jnp.mean(v, axis=1, keepdims=True)
        spread = jnp.mean(center * center, axis=1, keepdims=True)
        normed[at : at + 128, :] = center * lax.rsqrt(spread + EPS) * gain[...]

    def condition(i, noises):
        rows = slice(128 * i, 128 * i + 128)
        for m in range(4):
            terms = dot(noises(m), cond[...], 0, 0)
            hidden[m, rows, :] = (normed[rows, :] * (1.0 + terms[:, :1024]) + terms[:, 1024:]).astype(BF16)

    forward_y(0)
    for f in fetches[9:]:
        f.wait()
    normalise(states[0:128, :], 128)
    forward_y(1)
    forward_y(2)
    normalise(states[128:256, :], 256)
    forward_y(3)
    forward_y(4)
    forward_x()
    for part_of in range(2):
        row = lax.broadcasted_iota(jnp.int32, (256, 256), 0) + 256 * part_of
        total = jnp.zeros((256, 256), F32)
        for k in range(8):
            total = total + (row == edges[k : k + 1, :]).astype(F32)
        counts[256 * part_of : 256 * part_of + 256, :] = total
    forward_y(5)
    forward_y(6)
    forward_y(7)
    forward_core(0)
    forward_core(1)
    for t in (1, 2, 3):
        other = lax.rem(x + 4 - t, 4)
        slot = nown.at[other]
        remote(slot, slot, xs.at[t, 0], xr.at[t, 0], at_x(me, -t)).wait_recv()
    condition(1, lambda m: nown[m, :, 0:128])
    forward_core(2)
    condition(2, lambda m: nown[m, :, 128:256])
    forward_core(3)
    for t in (1, 2, 3):
        other = lax.rem(x + 4 - t, 4)
        slot = halo.at[:, pl.ds(pl.multiple_of(32 * other, 32), 32)]
        remote(slot, slot, xs.at[t, 1], xr.at[t, 1], at_x(me, -t)).wait_recv()
        slot = nhalo.at[other]
        remote(slot, slot, xs.at[t, 2], xr.at[t, 2], at_x(me, -t)).wait_recv()
    normalise(halo[0], 0)
    condition(0, lambda m: nhalo[m, 0])
    forward_core(4)
    normalise(halo[1], 384)
    condition(3, lambda m: nhalo[m, 1])
    forward_core(5)
    node = lax.broadcasted_iota(jnp.int32, (256, 1024), 0)
    select = jnp.zeros((256, 1024), F32)
    for k in range(3):
        select = select + jnp.where(node == source[k : k + 1, :], weight[k : k + 1, :], 0.0)
    wide[0] = select.astype(BF16)
    wide[1] = (select - wide[0].astype(F32)).astype(BF16)
    forward_core(6)
    tall[0:100, :] = truth[...].astype(F32)
    tall[100:128, :] = jnp.zeros((28, 1024), F32)
    base = dot(wd[...], states[...], 1, 1)
    scores[0:100, 0:256] = base
    scores[100:128, 0:256] = jnp.zeros((28, 256), F32)
    forward_core(7)
    for k, o in enumerate(order):
        landed = wall.at[lax.rem(z + 8 - o, 8), :, 1 - c]
        remote(landed, landed, cs.at[k], cr.at[k], at_core(me)).wait_recv()

    wvt[...] = wall[...].reshape(1024, 896)[:, 512:768].T
    w2t[...] = wall[pl.ds(2 * x, 2)].reshape(256, 896)[:, 768:896].T
    lane = lax.broadcasted_iota(jnp.int32, (256, 256), 1) // 64
    group = quarter

    def to_x(m, t):
        peer = at_x(me, t)
        there = pl.ds(pl.multiple_of(32 * peer[1], 32), 32)
        return remote(part.at[m, there], got.at[m, t], ps.at[m, t], pr.at[m, t], peer)

    def to_other(m):
        return remote(mine.at[m], theirs.at[m], fs.at[m], fr.at[m], at_y(me, 4))

    def combine(m):
        update = part[m, group, :].astype(F32)
        for t in (1, 2, 3):
            remote(got.at[m, t], got.at[m, t], ps.at[m, t], pr.at[m, t], at_x(me, -t)).wait_recv()
            update = update + got[m, t].astype(F32)
        mine[m] = update.astype(BF16)
        to_other(m).start()

    def member(m, _):
        all_rows = hidden[m]
        w = wall[...].reshape(1024, 896)
        query = dot(hidden[m, 128:384, :], w[:, 0:256], 1, 0).astype(BF16) * 0.125
        key = dot(all_rows, w[:, 256:512], 1, 0).astype(BF16)
        value_t = dot(wvt[...], all_rows, 1, 1).astype(BF16)
        for h in range(4):
            one = jnp.where(lane == h, query, jnp.zeros_like(query))
            score = dot(key, one, 1, 1)
            count = counts[...]
            score = jnp.where(count > 0.0, score, NEG)
            top = jnp.max(score, axis=0, keepdims=True)
            share = jnp.exp(score - top) * count
            below = jnp.sum(share, axis=0, keepdims=True)
            above = dot(value_t[64 * h : 64 * h + 64, :], share.astype(BF16), 1, 0)
            att[64 * h : 64 * h + 64, :] = (above / below).astype(BF16)
        part[m] = dot(w2t[...], att[...], 1, 0).astype(BF16)
        for t in (1, 2, 3):
            to_x(m, t).start()

        @pl.when(m > 0)
        def _():
            combine(m - 1)

        return 0

    lax.fori_loop(0, 4, member, 0)
    combine(3)
    base = scores[group, 0:256]

    def decode(held, at):
        whole = (base[None] + held[...].astype(F32)).reshape(128, 256)
        high = whole.astype(BF16)
        low = (whole - high.astype(F32)).astype(BF16)
        both = dot(jnp.concatenate([high, low], axis=0), wide[0], 1, 0)
        value = both[0:128] + both[128:256] + dot(high, wide[1], 1, 0)
        fields[at : at + 4] = value.astype(BF16).astype(F32).reshape(4, 32, 1024)

    decode(mine, 0)
    valid = lax.broadcasted_iota(jnp.int32, (32, 128), 0) + 32 * x < 100

    def inner(i, _):
        cols = pl.ds(pl.multiple_of(128 * i, 128), 128)
        y = tall[group, cols]
        f = [fields[m, :, cols] for m in range(4)]
        slope = [jnp.zeros((32, 128), F32) for _ in range(4)]
        spread = jnp.zeros((32, 128), F32)
        skill = jnp.zeros((32, 128), F32)
        for m in range(4):
            for n in range(m + 1, 4):
                d = f[m] - f[n]
                q = d * d + SMOOTH2
                r = lax.rsqrt(q)
                s = d * r
                slope[m] = slope[m] + s
                slope[n] = slope[n] - s
                spread = spread + q * r
        for m in range(4):
            d = f[m] - y
            q = d * d + SMOOTH2
            r = lax.rsqrt(q)
            skill = skill + q * r
            slopes[m, :, cols] = d * r - slope[m] * (1.0 / 7.0)
        scores[0:32, cols] = skill * (1.0 / 8.0) - spread * (2.0 / 112.0)
        return 0

    lax.fori_loop(0, 8, inner, 0)
    for m in range(4):
        remote(theirs.at[m], theirs.at[m], fs.at[m], fr.at[m], at_y(me, 4)).wait_recv()
    decode(theirs, 4)

    def across(i, carry):
        cols = pl.ds(pl.multiple_of(128 * i, 128), 128)
        a = area[:, cols]
        f = [fields[m, :, cols] for m in range(8)]
        spread = jnp.zeros((32, 128), F32)
        for m in range(4):
            slope = jnp.zeros((32, 128), F32)
            for n in range(4, 8):
                d = f[m] - f[n]
                q = d * d + SMOOTH2
                r = lax.rsqrt(q)
                slope = slope + d * r
                spread = spread + q * r
            made[m, :, cols] = (a * (slopes[m, :, cols] - slope * (1.0 / 7.0))).astype(BF16)
        score = a * (scores[0:32, cols] - spread * (1.0 / 112.0))
        return carry + jnp.where(valid, score, 0.0)

    total = lax.fori_loop(0, 8, across, jnp.zeros((32, 128), F32))
    l0[...] = total[0:8] + total[8:16] + total[16:24] + total[24:32]

    for t, peer in enumerate(plane):
        go(remote(l0, b1.at[t], ls.at[0, t], lr.at[0, t], peer))
    for t in (1, 2, 3):
        peer = at_x(me, t)
        go(remote(made.at[peer[1]], grad.at[group], gs.at[t], gr.at[t], peer))
    grad[group, :] = made[x]

    def collect(here, inbox, stage, sources):
        value = here[...]
        for t, peer in enumerate(sources):
            remote(inbox.at[t], inbox.at[t], ls.at[stage, t], lr.at[stage, t], peer).wait_recv()
            value = value + inbox[t]
        return value

    l1[...] = collect(l0, b1, 0, plane_from)
    for t in range(7):
        go(remote(l1, b2.at[t], ls.at[1, t], lr.at[1, t], at_z(me, t + 1)))
    l2[...] = collect(l1, b2, 1, [at_z(me, -t) for t in range(1, 8)])
    for t in range(7):
        go(remote(l2, b3.at[t], ls.at[2, t], lr.at[2, t], at_y(me, t + 1)))
    value = collect(l2, b3, 2, [at_y(me, -t) for t in range(1, 8)])
    value = jnp.sum(jnp.sum(value, axis=0, keepdims=True), axis=1, keepdims=True)
    loss[...] = value * (1.0 / 6553600.0)
    for t in (1, 2, 3):
        peer = at_x(me, -t)
        there = pl.ds(pl.multiple_of(32 * peer[1], 32), 32)
        remote(grad.at[there], grad.at[there], gs.at[t], gr.at[t], peer).wait_recv()
    for copy in started:
        copy.wait_send()
    for m in range(4):
        for t in (1, 2, 3):
            to_x(m, t).wait_send()
        to_other(m).wait_send()


def dma(*shape):
    return pltpu.SemaphoreType.DMA(shape)


def per_device(
    node_states, noise, norm_gain, cond_weight, w_query, w_key, w_value, w_out,
    edge_src, send_rows, dec_src, dec_weight, w_decode, truth, area,
):
    grad, loss = pl.pallas_call(
        step_kernel,
        out_shape=(
            jax.ShapeDtypeStruct((128, 1024), BF16),
            jax.ShapeDtypeStruct((1, 1), F32),
        ),
        in_specs=[pl.BlockSpec(memory_space=pl.ANY)] * 15,
        out_specs=(VMEM, VMEM),
        scratch_shapes=[
            pltpu.VMEM((256, 1024), BF16),
            pltpu.VMEM((16, 256), BF16),
            pltpu.VMEM((1, 256), jnp.int32),
            pltpu.VMEM((1, 1024), F32),
            pltpu.VMEM((16, 2048), BF16),
            pltpu.VMEM((8, 256), jnp.int32),
            pltpu.VMEM((100, 1024), BF16),
            pltpu.VMEM((3, 1024), jnp.int32),
            pltpu.VMEM((3, 1024), F32),
            pltpu.VMEM((100, 1024), BF16),
            pltpu.VMEM((1, 1024), F32),
            pltpu.VMEM((16, 1024), BF16),
            pltpu.VMEM((8, 4, 2, 16, 896), BF16),
            pltpu.VMEM((2, 128, 1024), BF16),
            pltpu.VMEM((4, 2, 16, 128), BF16),
            pltpu.VMEM((4, 16, 256), BF16),
            pltpu.VMEM((2, 128, 1024), BF16),
            pltpu.VMEM((2, 16, 128), BF16),
            pltpu.VMEM((512, 1024), F32),
            pltpu.VMEM((512, 256), F32),
            pltpu.VMEM((4, 512, 1024), BF16),
            pltpu.VMEM((256, 1024), BF16),
            pltpu.VMEM((128, 256), BF16),
            pltpu.VMEM((256, 256), BF16),
            pltpu.VMEM((4, 128, 256), BF16),
            pltpu.VMEM((4, 4, 32, 256), BF16),
            pltpu.VMEM((4, 32, 256), BF16),
            pltpu.VMEM((4, 32, 256), BF16),
            pltpu.VMEM((2, 256, 1024), BF16),
            pltpu.VMEM((128, 1024), F32),
            pltpu.VMEM((8, 32, 1024), F32),
            pltpu.VMEM((4, 32, 1024), F32),
            pltpu.VMEM((128, 1024), F32),
            pltpu.VMEM((4, 32, 1024), BF16),
            pltpu.VMEM((8, 128), F32),
            pltpu.VMEM((8, 128), F32),
            pltpu.VMEM((8, 128), F32),
            pltpu.VMEM((7, 8, 128), F32),
            pltpu.VMEM((7, 8, 128), F32),
            pltpu.VMEM((7, 8, 128), F32),
            dma(16),
            dma(8), dma(8), dma(8, 3), dma(8, 3), dma(8), dma(8), dma(2), dma(2), dma(2), dma(2),
            dma(4, 3), dma(4, 3), dma(4, 4), dma(4, 4), dma(4), dma(4), dma(4), dma(4),
            dma(3, 7), dma(3, 7),
        ],
        compiler_params=pltpu.CompilerParams(collective_id=0, has_side_effects=True),
        name="step",
    )(
        w_query, w_key, w_value, w_out, node_states, noise[0], send_rows.reshape(1, 256),
        norm_gain.reshape(1, 1024), cond_weight, edge_src, w_decode,
        dec_src, dec_weight, truth, area.reshape(1, 1024),
    )
    return loss[0, 0], grad[None, :100]


def solution(mesh):
    split = Mesh(mesh.devices.reshape(2, 4, 8, 4, 2), MEMBER + SPACE)
    return jax.shard_map(
        per_device,
        mesh=split,
        in_specs=(
            P(SPACE, None),
            P(MEMBER, None, SPACE),
            P(),
            P(),
            P(SPACE, None),
            P(SPACE, None),
            P(SPACE, None),
            P(SPACE, None),
            P(None, SPACE),
            P(SPACE),
            P(None, SPACE),
            P(None, SPACE),
            P(),
            P(None, SPACE),
            P(SPACE),
        ),
        out_specs=(P(), P(MEMBER, None, SPACE)),
        check_vma=False,
    )
```

time: 98.8 us -> 72.5 us (0.73)
  Pallas kernels: 84.1 us -> 68.3 us
  local copies, waits for them, and re-layouts: 11.3 us -> 1.63 us
    pallas_call x3 -> x1, Pallas kernels: 84.1 us -> 68.3 us  [per_device(): pl.pallas_call(step_kernel, out_shape=(jax.ShapeDtypeStruct((128, 1024),...]
    unnamed x18 -> x0, local copies, waits for them, and re-layouts: 8.02 us -> none
    pad x1 -> x0, local copies, waits for them, and re-layouts: 1.67 us -> none  [per_device(): decoder = jnp.pad(w_decode, ((0, 28), (0, 0)))]
where the time goes in v2:
time: 72.5 us; the launch traced here: 72.3 us
  Pallas kernels  68.3 us (94%)
  between operations  2.41 us (3%)
  local copies, waits for them, and re-layouts  1.63 us (2%)
    pallas_call x1, Pallas kernels, per_device(): pl.pallas_call(step_kernel, out_shape=(jax.ShapeDtypeStruct((128, 1024),...  68.3 us
    broadcast_in_dim x1, local copies, waits for them, and re-layouts, per_device(): return (loss[0, 0], grad[None, :100])  1.63 us

profile of v2, /device:TPU:1, one launch (start us, length us, event | category | flops | bytes accessed | tf_op | source)
XLA Modules:
  0.0 72.3 jit_solution(9314217707296132596)
XLA Ops:
  0.6 68.3 %step.1 = (bf16[128,1024]{1,0:T(8,128)(2,1)}, f32[1,1]{1,0:T(1,128)}) custom-call(bf16[16,1024]{1,0:T(8,128)(2,1)} %wq.1, bf16[16,1024]{1,0:T(8,128)(2,1)} %wk.1, bf16[16,1024]{1,0:T(8,128)(2,1)} %wv.1, bf16[16,1024]{1,0:T(8,128)(2,1)} %wo.1, bf16[256,1024]{1,0:T(8,128)(2,1)} %states_in.1, bf16[16,256]{1,0:T(8,128)(2,1)} %bitcast.7, s32[1,256]{1,0:T(1,128)} %bitcast.10, ...), custom_call_target="tpu_custom_call" | custom-call | tf_op jit(solution)/shard_map/step/pallas_call | solution.py:417
  68.9 1.6 %slice_bitcast_fusion = bf16[1,100,1024]{2,1,0:T(8,128)(2,1)} fusion(bf16[128,1024]{1,0:T(8,128)(2,1)} %get-tuple-element.5), kind=kLoop, calls=%fused_computation | loop fusion | bytes 409600 | tf_op jit(solution)/shard_map/broadcast_in_dim | solution.py:478

commit v3 on v2

--- a/solution.py
+++ b/solution.py
@@ -80,28 +80,24 @@
     states, noise, rows, gain, cond, edges, wd, source, weight, truth, area, wo_here,
     wall, halo, nhalo, nown, picked, npicked,
     normed, counts, hidden, wvt, w2t, att,
-    part, got, mine, theirs, wide, tall, fields, slopes, scores, made, l0, l1, l2, b1, b2, b3,
-    fetch, zs, zr, ys, yr, cs, cr, hs, hr, ns, nr, xs, xr, ps, pr, fs, fr, gs, gr, ls, lr,
+    part, got, mine, theirs, wide, tall, fields, slopes, scores, made, l0, l1, b1, b2,
+    fetch, zs, zr, ys, yr, cs, cr, hs, hr, ns, nr, xs, xr, ps, pr, fs, fr, gs, gr, ls, lr, zs2, zr2,
 ):
     me = place()
     yh, x, z, yl, c = me
-    plane = [
-        (yh, lax.rem(x + dx, 4), z, yl, lax.rem(c + dc, 2))
-        for dx in range(4)
-        for dc in range(2)
-        if dx or dc
-    ]
-    plane_from = [
-        (yh, lax.rem(x + 4 - dx, 4), z, yl, lax.rem(c + dc, 2))
-        for dx in range(4)
-        for dc in range(2)
-        if dx or dc
-    ]
+    spots = [(dx, dc, dy) for dy in (2, 1, -1, 0) for dx in range(4) for dc in range(2) if dx or dc or dy]
+
+    def near(dx, dc, dy):
+        yh_, _, _, yl_, _ = at_y(me, dy)
+        return (yh_, lax.rem(x + 4 + dx, 4), z, yl_, lax.rem(c + dc, 2))
+
     wait_all = greet(
         [at_z(me, o) for o in OFFSETS]
-        + [at_y(me, o) for o in range(1, 8)]
-        + plane
+        + [at_y(me, o) for o in (1, -1, 2, -2, 4)]
+        + [at_core(me)]
+        + [at_x(me, o) for o in (1, 2, 3)]
         + [at_block(me, 1), at_block(me, -1)]
+        + [near(-dx, dc, -dy) for dx, dc, dy in spots]
     )
     columns = pl.ds(pl.multiple_of(256 * x, 256), 256)
     own = wall.at[z, yl, c]
@@ -216,7 +212,9 @@
         total = jnp.zeros((256, 256), F32)
         for k in range(8):
             total = total + (row == edges[k : k + 1, :]).astype(F32)
-        counts[256 * part_of : 256 * part_of + 256, :] = total
+        counts[256 * part_of : 256 * part_of + 256, :] = jnp.where(
+            total > 0.0, jnp.log(jnp.maximum(total, 1.0)), NEG
+        )
     forward_y(5)
     forward_y(6)
     forward_y(7)
@@ -288,11 +286,9 @@
         value_t = dot(wvt[...], all_rows, 1, 1).astype(BF16)
         for h in range(4):
             one = jnp.where(lane == h, query, jnp.zeros_like(query))
-            score = dot(key, one, 1, 1)
-            count = counts[...]
-            score = jnp.where(count > 0.0, score, NEG)
+            score = dot(key, one, 1, 1) + counts[...]
             top = jnp.max(score, axis=0, keepdims=True)
-            share = jnp.exp(score - top) * count
+            share = jnp.exp(score - top)
             below = jnp.sum(share, axis=0, keepdims=True)
             above = dot(value_t[64 * h : 64 * h + 64, :], share.astype(BF16), 1, 0)
             att[64 * h : 64 * h + 64, :] = (above / below).astype(BF16)
@@ -310,90 +306,89 @@
     combine(3)
     base = scores[group, 0:256]
 
-    def decode(held, at):
-        whole = (base[None] + held[...].astype(F32)).reshape(128, 256)
+    def decode(held, first, count, at):
+        whole = (base[None] + held[first : first + count].astype(F32)).reshape(32 * count, 256)
         high = whole.astype(BF16)
         low = (whole - high.astype(F32)).astype(BF16)
         both = dot(jnp.concatenate([high, low], axis=0), wide[0], 1, 0)
-        value = both[0:128] + both[128:256] + dot(high, wide[1], 1, 0)
-        fields[at : at + 4] = value.astype(BF16).astype(F32).reshape(4, 32, 1024)
-
-    decode(mine, 0)
-    valid = lax.broadcasted_iota(jnp.int32, (32, 128), 0) + 32 * x < 100
-
-    def inner(i, _):
+        value = both[: 32 * count] + both[32 * count :] + dot(high, wide[1], 1, 0)
+        fields[at : at + count] = value.astype(BF16).astype(F32).reshape(count, 32, 1024)
+
+    def arrived(m):
+        remote(theirs.at[m], theirs.at[m], fs.at[m], fr.at[m], at_y(me, 4)).wait_recv()
+
+    def gap(d):
+        q = d * d + SMOOTH2
+        r = lax.rsqrt(q)
+        return d * r, q * r
+
+    decode(mine, 0, 4, 0)
+    for m in range(3):
+        arrived(m)
+    decode(theirs, 0, 3, 4)
+
+    def early(i, _):
         cols = pl.ds(pl.multiple_of(128 * i, 128), 128)
         y = tall[group, cols]
-        f = [fields[m, :, cols] for m in range(4)]
+        f = [fields[m, :, cols] for m in range(7)]
         slope = [jnp.zeros((32, 128), F32) for _ in range(4)]
         spread = jnp.zeros((32, 128), F32)
         skill = jnp.zeros((32, 128), F32)
-        for m in range(4):
-            for n in range(m + 1, 4):
-                d = f[m] - f[n]
-                q = d * d + SMOOTH2
-                r = lax.rsqrt(q)
-                s = d * r
-                slope[m] = slope[m] + s
-                slope[n] = slope[n] - s
-                spread = spread + q * r
-        for m in range(4):
-            d = f[m] - y
-            q = d * d + SMOOTH2
-            r = lax.rsqrt(q)
-            skill = skill + q * r
-            slopes[m, :, cols] = d * r - slope[m] * (1.0 / 7.0)
+        for m in range(7):
+            for n in range(m + 1, 7):
+                s, value = gap(f[m] - f[n])
+                spread = spread + value
+                if m < 4:
+                    slope[m] = slope[m] + s
+                if n < 4:
+                    slope[n] = slope[n] - s
+        for m in range(7):
+            s, value = gap(f[m] - y)
+            skill = skill + value
+            if m < 4:
+                slopes[m, :, cols] = s - slope[m] * (1.0 / 7.0)
         scores[0:32, cols] = skill * (1.0 / 8.0) - spread * (2.0 / 112.0)
         return 0
 
-    lax.fori_loop(0, 8, inner, 0)
-    for m in range(4):
-        remote(theirs.at[m], theirs.at[m], fs.at[m], fr.at[m], at_y(me, 4)).wait_recv()
-    decode(theirs, 4)
-
-    def across(i, carry):
+    lax.fori_loop(0, 8, early, 0)
+    valid = lax.broadcasted_iota(jnp.int32, (32, 128), 0) + 32 * x < 100
+    arrived(3)
+    decode(theirs, 3, 1, 7)
+
+    def late(i, carry):
         cols = pl.ds(pl.multiple_of(128 * i, 128), 128)
         a = area[:, cols]
-        f = [fields[m, :, cols] for m in range(8)]
+        last = fields[7, :, cols]
         spread = jnp.zeros((32, 128), F32)
-        for m in range(4):
-            slope = jnp.zeros((32, 128), F32)
-            for n in range(4, 8):
-                d = f[m] - f[n]
-                q = d * d + SMOOTH2
-                r = lax.rsqrt(q)
-                slope = slope + d * r
-                spread = spread + q * r
-            made[m, :, cols] = (a * (slopes[m, :, cols] - slope * (1.0 / 7.0))).astype(BF16)
-        score = a * (scores[0:32, cols] - spread * (1.0 / 112.0))
+        for m in range(7):
+            s, value = gap(fields[m, :, cols] - last)
+            spread = spread + value
+            if m < 4:
+                made[m, :, cols] = (a * (slopes[m, :, cols] - s * (1.0 / 7.0))).astype(BF16)
+        _, value = gap(last - tall[group, cols])
+        score = a * (scores[0:32, cols] + value * (1.0 / 8.0) - spread * (2.0 / 112.0))
         return carry + jnp.where(valid, score, 0.0)
 
-    total = lax.fori_loop(0, 8, across, jnp.zeros((32, 128), F32))
-    l0[...] = total[0:8] + total[8:16] + total[16:24] + total[24:32]
-
-    for t, peer in enumerate(plane):
-        go(remote(l0, b1.at[t], ls.at[0, t], lr.at[0, t], peer))
+    total = lax.fori_loop(0, 8, late, jnp.zeros((32, 128), F32))
+    l0[...] = jnp.sum(total, axis=0, keepdims=True)
+
+    for t, spot in enumerate(spots):
+        go(remote(l0, b1.at[t], ls.at[t], lr.at[t], near(*spot)))
     for t in (1, 2, 3):
         peer = at_x(me, t)
         go(remote(made.at[peer[1]], grad.at[group], gs.at[t], gr.at[t], peer))
-    grad[group, :] = made[x]
-
-    def collect(here, inbox, stage, sources):
-        value = here[...]
-        for t, peer in enumerate(sources):
-            remote(inbox.at[t], inbox.at[t], ls.at[stage, t], lr.at[stage, t], peer).wait_recv()
-            value = value + inbox[t]
-        return value
-
-    l1[...] = collect(l0, b1, 0, plane_from)
+    keep = pltpu.make_async_copy(made.at[x], grad.at[group], gs.at[0])
+    keep.start()
+    for t, (dx, dc, dy) in enumerate(spots):
+        remote(b1.at[t], b1.at[t], ls.at[t], lr.at[t], near(-dx, dc, -dy)).wait_recv()
+    l1[...] = l0[...] + jnp.sum(b1[...], axis=0)
     for t in range(7):
-        go(remote(l1, b2.at[t], ls.at[1, t], lr.at[1, t], at_z(me, t + 1)))
-    l2[...] = collect(l1, b2, 1, [at_z(me, -t) for t in range(1, 8)])
+        go(remote(l1, b2.at[t], zs2.at[t], zr2.at[t], at_z(me, t + 1)))
     for t in range(7):
-        go(remote(l2, b3.at[t], ls.at[2, t], lr.at[2, t], at_y(me, t + 1)))
-    value = collect(l2, b3, 2, [at_y(me, -t) for t in range(1, 8)])
-    value = jnp.sum(jnp.sum(value, axis=0, keepdims=True), axis=1, keepdims=True)
-    loss[...] = value * (1.0 / 6553600.0)
+        remote(b2.at[t], b2.at[t], zs2.at[t], zr2.at[t], at_z(me, -t - 1)).wait_recv()
+    value = l1[...] + jnp.sum(b2[...], axis=0)
+    loss[...] = jnp.sum(value, axis=1, keepdims=True) * (1.0 / 6553600.0)
+    keep.wait()
     for t in (1, 2, 3):
         peer = at_x(me, -t)
         there = pl.ds(pl.multiple_of(32 * peer[1], 32), 32)
@@ -421,7 +416,7 @@
             jax.ShapeDtypeStruct((1, 1), F32),
         ),
         in_specs=[pl.BlockSpec(memory_space=pl.ANY)] * 15,
-        out_specs=(VMEM, VMEM),
+        out_specs=(pl.BlockSpec(memory_space=pl.ANY), VMEM),
         scratch_shapes=[
             pltpu.VMEM((256, 1024), BF16),
             pltpu.VMEM((16, 256), BF16),
@@ -457,16 +452,14 @@
             pltpu.VMEM((4, 32, 1024), F32),
             pltpu.VMEM((128, 1024), F32),
             pltpu.VMEM((4, 32, 1024), BF16),
-            pltpu.VMEM((8, 128), F32),
-            pltpu.VMEM((8, 128), F32),
-            pltpu.VMEM((8, 128), F32),
-            pltpu.VMEM((7, 8, 128), F32),
-            pltpu.VMEM((7, 8, 128), F32),
-            pltpu.VMEM((7, 8, 128), F32),
+            pltpu.VMEM((1, 128), F32),
+            pltpu.VMEM((1, 128), F32),
+            pltpu.VMEM((31, 1, 128), F32),
+            pltpu.VMEM((7, 1, 128), F32),
             dma(16),
             dma(8), dma(8), dma(8, 3), dma(8, 3), dma(8), dma(8), dma(2), dma(2), dma(2), dma(2),
             dma(4, 3), dma(4, 3), dma(4, 4), dma(4, 4), dma(4), dma(4), dma(4), dma(4),
-            dma(3, 7), dma(3, 7),
+            dma(31), dma(31), dma(7), dma(7),
         ],
         compiler_params=pltpu.CompilerParams(collective_id=0, has_side_effects=True),
         name="step",

time: 72.5 us -> 69.3 us (0.956)
  Pallas kernels: 68.3 us -> 65 us
    pallas_call x1, Pallas kernels: 68.3 us -> 65 us  [per_device(): pl.pallas_call(step_kernel, out_shape=(jax.ShapeDtypeStruct((128, 1024),...]
where the time goes in v3:
time: 69.3 us; the launch traced here: 69.1 us
  Pallas kernels  65 us (94%)
  between operations  2.41 us (3%)
  local copies, waits for them, and re-layouts  1.63 us (2%)
    pallas_call x1, Pallas kernels, per_device(): pl.pallas_call(step_kernel, out_shape=(jax.ShapeDtypeStruct((128, 1024),...  65 us
    broadcast_in_dim x1, local copies, waits for them, and re-layouts, per_device(): return (loss[0, 0], grad[None, :100])  1.63 us

profile of v3, /device:TPU:1, one launch (start us, length us, event | category | flops | bytes accessed | tf_op | source)
XLA Modules:
  0.0 69.1 jit_solution(14563128427541891196)
XLA Ops:
  0.6 65.0 %step.1 = (bf16[128,1024]{1,0:T(8,128)(2,1)}, f32[1,1]{1,0:T(1,128)}) custom-call(bf16[16,1024]{1,0:T(8,128)(2,1)} %wq.1, bf16[16,1024]{1,0:T(8,128)(2,1)} %wk.1, bf16[16,1024]{1,0:T(8,128)(2,1)} %wv.1, bf16[16,1024]{1,0:T(8,128)(2,1)} %wo.1, bf16[256,1024]{1,0:T(8,128)(2,1)} %states_in.1, bf16[16,256]{1,0:T(8,128)(2,1)} %bitcast.7, s32[1,256]{1,0:T(1,128)} %bitcast.10, ...), custom_call_target="tpu_custom_call" | custom-call | tf_op jit(solution)/shard_map/step/pallas_call | solution.py:412
  65.7 1.6 %slice_bitcast_fusion = bf16[1,100,1024]{2,1,0:T(8,128)(2,1)} fusion(bf16[128,1024]{1,0:T(8,128)(2,1)} %get-tuple-element.5), kind=kLoop, calls=%fused_computation | loop fusion | bytes 409600 | tf_op jit(solution)/shard_map/broadcast_in_dim | solution.py:471

commit v4 on v3

--- a/solution.py
+++ b/solution.py
@@ -15,6 +15,7 @@
 F32 = jnp.float32
 BF16 = jnp.bfloat16
 NEG = -1e30
+LARGEST = jnp.finfo(jnp.bfloat16).max
 VMEM = pl.BlockSpec(memory_space=pltpu.VMEM)
 
 OFFSETS = (1, 7, 2, 6, 3, 5, 4)
@@ -207,14 +208,11 @@
     forward_y(3)
     forward_y(4)
     forward_x()
-    for part_of in range(2):
-        row = lax.broadcasted_iota(jnp.int32, (256, 256), 0) + 256 * part_of
-        total = jnp.zeros((256, 256), F32)
-        for k in range(8):
-            total = total + (row == edges[k : k + 1, :]).astype(F32)
-        counts[256 * part_of : 256 * part_of + 256, :] = jnp.where(
-            total > 0.0, jnp.log(jnp.maximum(total, 1.0)), NEG
-        )
+    row = lax.broadcasted_iota(jnp.int32, (512, 256), 0)
+    total = jnp.zeros((512, 256), F32)
+    for k in range(8):
+        total = total + (row == edges[k : k + 1, :]).astype(F32)
+    counts[...] = jnp.where(total > 0.0, jnp.log(jnp.maximum(total, 1.0)), NEG).T
     forward_y(5)
     forward_y(6)
     forward_y(7)
@@ -257,7 +255,6 @@
         landed = wall.at[lax.rem(z + 8 - o, 8), :, 1 - c]
         remote(landed, landed, cs.at[k], cr.at[k], at_core(me)).wait_recv()
 
-    wvt[...] = wall[...].reshape(1024, 896)[:, 512:768].T
     w2t[...] = wall[pl.ds(2 * x, 2)].reshape(256, 896)[:, 768:896].T
     lane = lax.broadcasted_iota(jnp.int32, (256, 256), 1) // 64
     group = quarter
@@ -283,16 +280,17 @@
         w = wall[...].reshape(1024, 896)
         query = dot(hidden[m, 128:384, :], w[:, 0:256], 1, 0).astype(BF16) * 0.125
         key = dot(all_rows, w[:, 256:512], 1, 0).astype(BF16)
-        value_t = dot(wvt[...], all_rows, 1, 1).astype(BF16)
+        value = dot(all_rows, w[:, 512:768], 1, 0).astype(BF16)
         for h in range(4):
             one = jnp.where(lane == h, query, jnp.zeros_like(query))
-            score = dot(key, one, 1, 1) + counts[...]
-            top = jnp.max(score, axis=0, keepdims=True)
-            share = jnp.exp(score - top)
-            below = jnp.sum(share, axis=0, keepdims=True)
-            above = dot(value_t[64 * h : 64 * h + 64, :], share.astype(BF16), 1, 0)
-            att[64 * h : 64 * h + 64, :] = (above / below).astype(BF16)
-        part[m] = dot(w2t[...], att[...], 1, 0).astype(BF16)
+            share = jnp.exp(dot(one, key, 1, 1) + counts[...])
+            below = jnp.sum(share, axis=1, keepdims=True)
+            rounded = jnp.minimum(share.astype(BF16), LARGEST)
+            above = dot(rounded, value, 1, 0) / below
+            if h:
+                above = jnp.where(lane == h, above, att[...])
+            att[...] = above
+        part[m] = dot(w2t[...], att[...].astype(BF16), 1, 1).astype(BF16)
         for t in (1, 2, 3):
             to_x(m, t).start()
 
@@ -437,11 +435,11 @@
             pltpu.VMEM((2, 128, 1024), BF16),
             pltpu.VMEM((2, 16, 128), BF16),
             pltpu.VMEM((512, 1024), F32),
-            pltpu.VMEM((512, 256), F32),
+            pltpu.VMEM((256, 512), F32),
             pltpu.VMEM((4, 512, 1024), BF16),
-            pltpu.VMEM((256, 1024), BF16),
+            pltpu.VMEM((16, 128), BF16),
             pltpu.VMEM((128, 256), BF16),
-            pltpu.VMEM((256, 256), BF16),
+            pltpu.VMEM((256, 256), F32),
             pltpu.VMEM((4, 128, 256), BF16),
             pltpu.VMEM((4, 4, 32, 256), BF16),
             pltpu.VMEM((4, 32, 256), BF16),

time: 69.3 us -> 66.5 us (0.960)
  Pallas kernels: 65 us -> 62.3 us
    pallas_call x1, Pallas kernels: 65 us -> 62.3 us  [per_device(): pl.pallas_call(step_kernel, out_shape=(jax.ShapeDtypeStruct((128, 1024),...]
where the time goes in v4:
time: 66.5 us; the launch traced here: 66.3 us
  Pallas kernels  62.3 us (94%)
  between operations  2.41 us (4%)
  local copies, waits for them, and re-layouts  1.63 us (2%)
    pallas_call x1, Pallas kernels, per_device(): pl.pallas_call(step_kernel, out_shape=(jax.ShapeDtypeStruct((128, 1024),...  62.3 us
    broadcast_in_dim x1, local copies, waits for them, and re-layouts, per_device(): return (loss[0, 0], grad[None, :100])  1.63 us

profile of v4, /device:TPU:1, one launch (start us, length us, event | category | flops | bytes accessed | tf_op | source)
XLA Modules:
  0.0 66.3 jit_solution(6383655822886519549)
XLA Ops:
  0.6 62.3 %step.1 = (bf16[128,1024]{1,0:T(8,128)(2,1)}, f32[1,1]{1,0:T(1,128)}) custom-call(bf16[16,1024]{1,0:T(8,128)(2,1)} %wq.1, bf16[16,1024]{1,0:T(8,128)(2,1)} %wk.1, bf16[16,1024]{1,0:T(8,128)(2,1)} %wv.1, bf16[16,1024]{1,0:T(8,128)(2,1)} %wo.1, bf16[256,1024]{1,0:T(8,128)(2,1)} %states_in.1, bf16[16,256]{1,0:T(8,128)(2,1)} %bitcast.7, s32[1,256]{1,0:T(1,128)} %bitcast.10, ...), custom_call_target="tpu_custom_call" | custom-call | tf_op jit(solution)/shard_map/step/pallas_call | solution.py:410
  63.0 1.6 %slice_bitcast_fusion = bf16[1,100,1024]{2,1,0:T(8,128)(2,1)} fusion(bf16[128,1024]{1,0:T(8,128)(2,1)} %get-tuple-element.5), kind=kLoop, calls=%fused_computation | loop fusion | bytes 409600 | tf_op jit(solution)/shard_map/broadcast_in_dim | solution.py:469

commit v5 on v4

--- a/solution.py
+++ b/solution.py
@@ -15,6 +15,7 @@
 F32 = jnp.float32
 BF16 = jnp.bfloat16
 NEG = -1e30
+SCALE = 0.125 * 1.4426950408889634
 LARGEST = jnp.finfo(jnp.bfloat16).max
 VMEM = pl.BlockSpec(memory_space=pltpu.VMEM)
 
@@ -212,7 +213,7 @@
     total = jnp.zeros((512, 256), F32)
     for k in range(8):
         total = total + (row == edges[k : k + 1, :]).astype(F32)
-    counts[...] = jnp.where(total > 0.0, jnp.log(jnp.maximum(total, 1.0)), NEG).T
+    counts[...] = jnp.where(total > 0.0, jnp.log2(jnp.maximum(total, 1.0)), NEG).T
     forward_y(5)
     forward_y(6)
     forward_y(7)
@@ -278,12 +279,12 @@
     def member(m, _):
         all_rows = hidden[m]
         w = wall[...].reshape(1024, 896)
-        query = dot(hidden[m, 128:384, :], w[:, 0:256], 1, 0).astype(BF16) * 0.125
+        query = (dot(hidden[m, 128:384, :], w[:, 0:256], 1, 0) * SCALE).astype(BF16)
         key = dot(all_rows, w[:, 256:512], 1, 0).astype(BF16)
         value = dot(all_rows, w[:, 512:768], 1, 0).astype(BF16)
         for h in range(4):
             one = jnp.where(lane == h, query, jnp.zeros_like(query))
-            share = jnp.exp(dot(one, key, 1, 1) + counts[...])
+            share = jnp.exp2(dot(one, key, 1, 1) + counts[...])
             below = jnp.sum(share, axis=1, keepdims=True)
             rounded = jnp.minimum(share.astype(BF16), LARGEST)
             above = dot(rounded, value, 1, 0) / below

time: 66.5 us -> 66.5 us (level)
  no operation moved by 1% of the time
where the time goes in v5:
time: 66.5 us; the launch traced here: 66.4 us
  Pallas kernels  62.3 us (94%)
  between operations  2.41 us (4%)
  local copies, waits for them, and re-layouts  1.63 us (2%)
    pallas_call x1, Pallas kernels, per_device(): pl.pallas_call(step_kernel, out_shape=(jax.ShapeDtypeStruct((128, 1024),...  62.3 us
    broadcast_in_dim x1, local copies, waits for them, and re-layouts, per_device(): return (loss[0, 0], grad[None, :100])  1.63 us

profile of v5, /device:TPU:1, one launch (start us, length us, event | category | flops | bytes accessed | tf_op | source)
XLA Modules:
  0.0 66.4 jit_solution(3773373901476261239)
XLA Ops:
  0.6 62.3 %step.1 = (bf16[128,1024]{1,0:T(8,128)(2,1)}, f32[1,1]{1,0:T(1,128)}) custom-call(bf16[16,1024]{1,0:T(8,128)(2,1)} %wq.1, bf16[16,1024]{1,0:T(8,128)(2,1)} %wk.1, bf16[16,1024]{1,0:T(8,128)(2,1)} %wv.1, bf16[16,1024]{1,0:T(8,128)(2,1)} %wo.1, bf16[256,1024]{1,0:T(8,128)(2,1)} %states_in.1, bf16[16,256]{1,0:T(8,128)(2,1)} %bitcast.7, s32[1,256]{1,0:T(1,128)} %bitcast.10, ...), custom_call_target="tpu_custom_call" | custom-call | tf_op jit(solution)/shard_map/step/pallas_call | solution.py:411
  63.0 1.6 %slice_bitcast_fusion = bf16[1,100,1024]{2,1,0:T(8,128)(2,1)} fusion(bf16[128,1024]{1,0:T(8,128)(2,1)} %get-tuple-element.5), kind=kLoop, calls=%fused_computation | loop fusion | bytes 409600 | tf_op jit(solution)/shard_map/broadcast_in_dim | solution.py:470
